TPU v7x, 32 devices: a whole 2x2x4 slice. The times are simulated.
32 devices in a mesh: seq: 8 (over y, x, core), zero: 4 (over z).
Axes of the slice: x: 2, y: 2, z: 4, core: 2. Of those that a mesh axis runs over, the one named last changes fastest.
Arguments:
- hidden: bfloat16 [4, 1024, 1280], P('zero', 'seq'), may hold values from -6 to 6
- output_grad: bfloat16 [4, 1024, 2560], P('zero', 'seq'), may hold values from -6 to 6
- input_weight: bfloat16 [1280, 2856], P('zero'), may hold values from -0.15625 to 0.15625
- step_bias: float32 [40], replicated, may hold values from -7 to -2
- decay_log: float32 [40], replicated, may hold values from -4 to 1
- skip_gain: float32 [40], replicated, may hold values from 0.5 to 1.5
Outputs:
- hidden_grad: bfloat16 [4, 1024, 1280], P('zero', 'seq')
- weight_grad: float32 [1280, 2856], P(('seq', 'zero'))
- head_grads: float32 [3, 40], replicated
All inputs are finite; a program needn't handle non-finite values.
Results may differ from a plain program's by a relative error of at most 0.0049.
Values may be sent and summed in bfloat16 or wider, within the bound.
A program may use at most 192 MiB of HBM per device.

v0:
```python
import jax
import jax.numpy as jnp
from jax import lax
from jax.sharding import PartitionSpec as P

HEADS = 40
HEAD_DIM = 64
STATE = 128
GROUP = 128
INNER = 2560


highest = lax.Precision.HIGHEST


def prefix(part, axis, combine, identity, reverse):
    count = lax.axis_size(axis)
    place = lax.axis_index(axis)
    ahead = count - 1 - place if reverse else place
    gathered = jax.tree.map(lambda a: lax.all_gather(a, axis), part)
    state = jax.tree.map(lambda a, e: jnp.zeros_like(a) + jnp.asarray(e, a.dtype), part, identity)

    def one(step, state):
        source = count - 1 - step if reverse else step
        return combine(
            state, jax.tree.map(lambda a: lax.dynamic_index_in_dim(a, source, 0, False), gathered)
        )

    return lax.fori_loop(0, ahead, one, state)


def state_mixer(columns, step_bias, decay_log, skip_gain, initial):
    length = columns.shape[0]
    blocks = length // GROUP
    values = jax.nn.silu(columns[:, :INNER])
    input_map = jax.nn.silu(columns[:, INNER : INNER + STATE]).reshape(blocks, GROUP, STATE)
    output_map = jax.nn.silu(columns[:, INNER + STATE : INNER + 2 * STATE]).reshape(
        blocks, GROUP, STATE
    )
    step_size = jax.nn.softplus(columns[:, INNER + 2 * STATE :] + step_bias)
    log_decay = -jnp.exp(decay_log) * step_size
    head_values = values.reshape(blocks, GROUP, HEADS, HEAD_DIM)
    scaled = head_values * step_size.reshape(blocks, GROUP, HEADS)[:, :, :, None]
    cumulative = jnp.cumsum(log_decay.reshape(blocks, GROUP, HEADS), axis=1)
    causal = (
        lax.broadcasted_iota(jnp.int32, (GROUP, GROUP), 0)
        >= lax.broadcasted_iota(jnp.int32, (GROUP, GROUP), 1)
    )[None, :, :, None]
    differences = cumulative[:, :, None, :] - cumulative[:, None, :, :]
    within = jnp.where(causal, jnp.exp(jnp.where(causal, differences, 0.0)), 0.0)
    scores = jnp.einsum("kqn,ksn->kqs", output_map, input_map, precision=highest)
    inside = jnp.einsum(
        "kqsh,kshp->kqhp", scores[:, :, :, None] * within, scaled, precision=highest
    )
    tail_decay = jnp.exp(cumulative[:, -1:, :] - cumulative)
    group_states = jnp.einsum(
        "kshp,ksn->khpn", scaled * tail_decay[:, :, :, None], input_map, precision=highest
    )
    totals = cumulative[:, -1, :]

    def advance(running, inputs):
        block_total, block_state = inputs
        return (jnp.exp(block_total)[:, None, None] * running + block_state, running)

    final_state, entering = lax.scan(advance, initial, (totals, group_states))
    from_state = (
        jnp.einsum("kqn,khpn->kqhp", output_map, entering, precision=highest)
        * jnp.exp(cumulative)[:, :, :, None]
    )
    mixed_out = inside + from_state + skip_gain[None, None, :, None] * head_values
    return (mixed_out.reshape(length, INNER), final_state, jnp.sum(totals, axis=0))


def combine_states(earlier, later):
    return (earlier[0] + later[0], jnp.exp(later[0])[:, None, None] * earlier[1] + later[1])


def body(hidden, output_grad, input_weight, step_bias, decay_log, skip_gain):
    tokens = hidden[0]
    cotangent = output_grad[0].astype(jnp.float32)
    columns = tokens
    projected = jnp.dot(
        columns,
        lax.all_gather(input_weight, "zero", axis=0, tiled=True),
        preferred_element_type=jnp.float32,
    )
    initial = jnp.zeros((HEADS, HEAD_DIM, STATE), jnp.float32)
    unused, local_state, local_decay = state_mixer(
        projected, step_bias, decay_log, skip_gain, initial
    )
    identity = (jnp.zeros((HEADS,), jnp.float32), initial)
    before_decay, entering = prefix(
        (local_decay, local_state), "seq", combine_states, identity, False
    )

    def from_start(start_state):
        return state_mixer(projected, step_bias, decay_log, skip_gain, start_state)[0]

    unused_out, start_pull = jax.vjp(from_start, initial)
    direct = start_pull(cotangent)[0]
    after_decay, leaving_grad = prefix((local_decay, direct), "seq", combine_states, identity, True)

    def local_pass(columns, bias_part, log_part, gain_part, start_state):
        results = state_mixer(columns, bias_part, log_part, gain_part, start_state)
        return (results[0], results[1])

    unused_pair, pullback = jax.vjp(
        local_pass, projected, step_bias, decay_log, skip_gain, entering
    )
    column_grad, bias_grad, log_grad, gain_grad, unused_grad = pullback((cotangent, leaving_grad))
    rounded = column_grad.astype(jnp.bfloat16)
    head_grads = lax.psum(jnp.stack([bias_grad, log_grad, gain_grad]), ("seq", "zero"))
    token_grad = lax.dot_general(
        rounded,
        lax.all_gather(input_weight, "zero", axis=0, tiled=True),
        (((1,), (1,)), ((), ())),
        preferred_element_type=jnp.float32,
    )
    columns = tokens
    partial_rows = lax.psum_scatter(
        lax.dot_general(
            columns, rounded, (((0,), (0,)), ((), ())), preferred_element_type=jnp.float32
        ),
        "seq",
        scatter_dimension=0,
        tiled=True,
    )
    weight_grad = lax.psum_scatter(partial_rows, "zero", scatter_dimension=0, tiled=True)
    return (token_grad.astype(jnp.bfloat16)[None], weight_grad, head_grads)


def solution(mesh):
    placed = (P("zero", "seq", None), P("zero", "seq", None), P("zero", None), P(), P(), P())
    return jax.shard_map(
        body,
        mesh=mesh,
        in_specs=placed,
        out_specs=(P("zero", "seq", None), P(("seq", "zero"), None), P()),
        check_vma=False,
    )
```

profile of v0, /device:TPU:9, one launch (start us, length us, event | category | flops | bytes accessed | tf_op | source)
XLA Modules:
  0.0 582.5 jit_solution(8779042528322891402)
XLA Ops:
  7.2 0.7 all-gather.7.cloned.1.call-update
  8.0 0.3 copy-done.11
  8.3 0.3 copy.77
  8.7 134.8 %all-gather.7.cloned.1.call-done = bf16[1280,2856]{1,0:T(8,128)(2,1)} async-done(((bf16[320,2856]{1,0:T(8,128)(2,1)}), bf16[1280,2856]{1,0:T(8,128)(2,1)}) %all-gather.7.cloned.1.call-update) | async-done | bytes 7311376 | tf_op jit(solution)/shard_map/all_gather | solution.py:84
  143.5 6.2 %fusion.35 = f32[128,2856]{0,1:T(8,128)S(1)} fusion(bf16[1280,2856]{1,0:T(8,128)(2,1)} %all-gather.7.cloned.1.call-done, bf16[1,128,1280]{2,1,0:T(8,128)(2,1)S(1)} %copy-done), kind=kOutput, calls=%fused_computation.61 | convolution fusion | flops 935854080 | bytes 9101312 | tf_op jit(solution)/shard_map/dot_general | solution.py:82
  149.7 1.2 copy-done.7
  151.6 1.1 copy-done.2
  152.7 3.1 convolution_add_fusion.1
  156.0 9.4 %all-gather = f32[8,1,40]{2,1,0:T(1,128)S(1)} all-gather(f32[1,1,40]{2,1,0:T(1,128)S(1)} %get-tuple-element.256), channel_id=2, replica_groups=mesh['seq'=8,'zero'=4] {'seq'}, dimensions={0}, use_global_device_ids=true | all-gather | bytes 1440 | tf_op jit(solution)/shard_map/all_gather | solution.py:20
  165.5 1.2 fusion.58
  166.7 54.0 %all-gather.9.cloned.1.call-done = f32[320,64,128]{2,1,0:T(8,128)} async-done(((f32[40,64,128]{2,1,0:T(8,128)}), f32[320,64,128]{2,1,0:T(8,128)}) %all-gather.9.cloned.1.call-update) | async-done | bytes 10485776 | tf_op jit(solution)/shard_map/all_gather | solution.py:20
  220.8 9.7 %while.16 = (s32[]{:T(128)}, f32[40,64,128]{2,1,0:T(8,128)S(1)}, s32[]{:T(128)}, f32[8,40]{1,0:T(8,128)S(1)}, f32[8,40,64,128]{3,2,1,0:T(8,128)}, /*index=5*/s32[]{:T(128)}, s32[]{:T(128)}, s32[]{:T(128)}, s32[]{:T(128)}) while((s32[]{:T(128)}, f32[40,64,128]{2,1,0:T(8,128)S(1)}, s32[]{:T(128)}, f32[8,40]{1,0:T(8,128)S(1)}, ...), condition=%wide.region_2.3_spmd, body=%wide.region_1.2_spmd.sunk | while | flops 655366 | bytes 3932795 | solution.py:29
  220.8 1.6 bitcast_add_fusion.6
  222.5 1.6 bitcast_add_fusion.6
  224.1 1.6 bitcast_add_fusion.6
  225.7 1.6 bitcast_add_fusion.6
  227.3 1.6 bitcast_add_fusion.6
  229.0 1.6 bitcast_add_fusion.6
  230.6 2.0 convolution_bitcast_fusion.1
  232.7 3.3 multiply_add_fusion
  235.9 2.9 fusion.21
  238.9 1.1 copy-done.4
  240.0 2.3 convolution_add_fusion
  242.7 4.8 fusion.12
  247.5 2.4 multiply_reduce_fusion
  250.2 1.1 convolution_bitcast_fusion.2
  251.3 3.7 fusion.40
  255.0 51.3 %all-gather.11.cloned.1.call-done = f32[320,64,128]{2,1,0:T(8,128)} async-done(((f32[40,64,128]{2,1,0:T(8,128)}), f32[320,64,128]{2,1,0:T(8,128)}) %all-gather.11.cloned.1.call-update) | async-done | bytes 10485776 | tf_op jit(solution)/shard_map/all_gather | solution.py:20
  306.5 1.8 while.17
  306.5 1.6 bitcast_add_fusion.7
  308.3 0.4 multiply_reduce_fusion.1
  308.7 0.9 copy-done.3
  309.6 2.2 convolution_bitcast_fusion.4
  311.9 2.2 fusion.30
  314.1 1.1 fusion.38
  315.3 1.1 reduce_window_sum.32
  316.5 0.9 fusion.65
  317.5 7.2 %convolution_bitcast_fusion = f32[1280,2856]{0,1:T(8,128)} fusion(bf16[1,128,1280]{2,1,0:T(8,128)(2,1)S(1)} %copy-done, f32[128,2560]{0,1:T(8,128)S(1)} %copy-done.10, f32[128,128]{0,1:T(8,128)S(1)} %fusion.40, f32[128,128]{0,1:T(8,128)S(1)} %fusion.38, f32[128,40]{0,1:T(8,128)S(1)} %get-tuple-element.249), kind=kOutput, calls=%fused_computation.4 | convolution fusion | flops 937316352 | bytes 16412672 | tf_op jit(solution)/shard_map/dot_general | solution.py:121
  324.7 15.2 %copy.101 = f32[1280,2856]{1,0:T(8,128)} copy(f32[1280,2856]{0,1:T(8,128)} %convolution_bitcast_fusion) | data formatting | bytes 29245440
  340.0 115.8 %reduce-scatter.5.cloned.1.call-done = f32[160,2856]{1,0:T(8,128)} async-done(((f32[1280,2856]{1,0:T(8,128)}), f32[160,2856]{1,0:T(8,128)}) %reduce-scatter.5.cloned.1.call-update) | async-done | bytes 1827856
  455.8 3.3 copy.102
  459.2 0.6 copy-done.15
  459.8 0.6 dynamic-slice.4
  461.2 45.0 %psum.7 = f32[3,40]{1,0:T(4,128)} all-reduce(f32[3,40]{1,0:T(4,128)S(1)} %pad_maximum_fusion), channel_id=1, replica_groups=mesh['seq'=8,'zero'=4] {'seq','zero'}, use_global_device_ids=true, to_apply=%region_20.21 | all-reduce | flops 120 | bytes 960 | tf_op jit(solution)/shard_map/psum | solution.py:112
  506.2 6.1 %fusion.10 = bf16[1,128,1280]{2,1,0:T(8,128)(2,1)} fusion(bf16[1280,2856]{1,0:T(8,128)(2,1)} %all-gather.7.cloned.1.call-done, f32[128,2560]{0,1:T(8,128)S(1)} %copy-done.10, f32[128,128]{0,1:T(8,128)S(1)} %fusion.40, f32[128,128]{0,1:T(8,128)S(1)} %fusion.38, f32[128,40]{0,1:T(8,128)S(1)} %get-tuple-element.249), kind=kOutput, calls=%fused_computation.19 | convolution fusion | flops 937480192 | bytes 9101312 | tf_op jit(solution)/shard_map/dot_general | solution.py:113
  512.3 60.1 %all-reduce.9.cloned.1.call-done = f32[160,2856]{0,1:T(8,128)} async-done(((f32[160,2856]{0,1:T(8,128)}), f32[160,2856]{0,1:T(8,128)}) %all-reduce.9.cloned.1.call-update) | async-done | bytes 1827856
  572.5 2.3 constant_dynamic-slice_fusion
  574.8 1.2 copy.92
  (69 shorter events, 2.6 us)
Async XLA Ops:
  7.2 136.4 %copy-start = (bf16[1,128,1280]{2,1,0:T(8,128)(2,1)S(1)}, bf16[1,128,1280]{2,1,0:T(8,128)(2,1)}, u32[]{:S(2)}) copy-start(bf16[1,128,1280]{2,1,0:T(8,128)(2,1)} %param.10) | copy-start | bytes 983044
  7.2 1.1 copy-start.11
  7.2 1.5 copy-start.14
  7.2 136.3 %all-gather.7.cloned.1.call-start = ((), (), s32[]{:S(2)}) async-start(), calls=%async_computation.1 | async-start | bytes 9420800 | tf_op jit(solution)/shard_map/all_gather | solution.py:84
  7.9 212.7 %all-gather.9.cloned.1.call-start = ((), (), s32[]{:S(2)}) async-start(), calls=%async_computation.2 | async-start | bytes 11796480 | tf_op jit(solution)/shard_map/all_gather | solution.py:20
  8.7 224.0 %copy-start.5 = (bf16[1,128,2560]{1,2,0:T(8,128)(2,1)}, bf16[1,128,2560]{1,2,0:T(8,128)(2,1)S(1)}, u32[]{:S(2)}) copy-start(bf16[1,128,2560]{1,2,0:T(8,128)(2,1)S(1)} %copy.77) | copy-start | bytes 1966084
  8.7 142.3 %copy-start.12 = (f32[40]{0:T(128)S(1)}, f32[40]{0:T(128)}, u32[]{:S(2)}) copy-start(f32[40]{0:T(128)} %param.13) | copy-start | bytes 484
  149.7 1.2 copy-start.7
  151.6 1.1 copy-start.2
  155.8 150.5 %all-gather.11.cloned.1.call-start = ((), (), s32[]{:S(2)}) async-start(), calls=%async_computation.3 | async-start | bytes 11796480 | tf_op jit(solution)/shard_map/all_gather | solution.py:20
  230.5 2.1 copy-start.13
  232.6 3.3 copy-start.9
  232.6 3.3 copy-start.8
  238.9 1.1 copy-start.4
  242.3 213.5 %reduce-scatter.5.cloned.1.call-start = ((), (), s32[]{:S(2)}) async-start(), calls=%async_computation.4 | async-start | bytes 16957440
  308.3 1.3 copy-start.3
  309.6 2.2 copy-start.6
  311.9 5.6 copy-start.10
  339.9 232.5 %all-reduce.9.cloned.1.call-start = ((), (), s32[]{:S(2)}) async-start(), calls=%async_computation.5 | async-start | bytes 5849088
  459.1 0.7 copy-start.15
  572.5 3.5 copy-start.1
Sparse Core Ops, SparseCore 0:
  9.6 133.9 all-gather.6
  156.0 64.6 all-gather.8
  242.5 63.8 all-gather.10
  340.0 115.7 reduce-scatter.4
  459.3 113.1 all-reduce.8
where the time goes:
time: 588 us; the launch traced here: 583 us
  waiting for transfers between devices  417 us (71%)
  blocking collectives  54.4 us (9%)
  matrix products  46.5 us (8%)
  local copies, waits for them, and re-layouts  29.6 us (5%)
  other arithmetic  19.6 us (3%)
  between operations  14.8 us (3%)
    unnamed x7, waiting for transfers between devices  177 us
    all_gather x1, waiting for transfers between devices, body(): lax.all_gather(input_weight, 'zero', axis=0, tiled=True)  135 us
    all_gather x2, waiting for transfers between devices, prefix(): gathered = jax.tree.map(lambda a: lax.all_gather(a, axis), part)  105 us
    psum x1, blocking collectives, body(): lax.psum(jnp.stack([bias_grad, log_grad, gain_grad]), ('seq', 'zero'))  45 us
    unnamed x38, local copies, waits for them, and re-layouts  28.4 us
  transfers between devices with their start and end apart: 5, of which 5 were waited for; matrix products, arithmetic and copies ran while one was open for 4% of the time, Pallas kernels for 0%

commit v1 on v0

v1 whole, which is shorter than its diff:
```python
import functools

import jax
import jax.numpy as jnp
from jax import lax
from jax.experimental import pallas as pl
from jax.experimental.pallas import tpu as pltpu
from jax.sharding import PartitionSpec as P

HEAD_DIM = 64
STATE = 128
MESH = pl.DeviceIdType.MESH
F32 = jnp.float32
BF16 = jnp.bfloat16


def up(size, unit):
    return -(-size // unit) * unit


def nn(a, b):
    return lax.dot_general(a, b, (((1,), (0,)), ((), ())), preferred_element_type=F32)


def nt(a, b):
    return lax.dot_general(a, b, (((1,), (1,)), ((), ())), preferred_element_type=F32)


def tn(a, b):
    return lax.dot_general(a, b, (((0,), (0,)), ((), ())), preferred_element_type=F32)


def exact(a, b):
    return lax.dot_general(
        a, b, (((1,), (0,)), ((), ())), precision=lax.Precision.HIGHEST, preferred_element_type=F32
    )


def greet(peers):
    barrier = pltpu.get_barrier_semaphore()
    total = 0
    for count, peer in peers:

        def one(step, carry, peer=peer):
            pl.semaphore_signal(barrier, inc=1, device_id=peer(step), device_id_type=MESH)
            return carry

        lax.fori_loop(1, count, one, 0)
        total += count - 1
    pl.semaphore_wait(barrier, total)


def run_copies(copies, locals_):
    for copy in locals_:
        copy.start()
    for count, make in copies:
        lax.fori_loop(1, count, lambda step, c, make=make: (make(step).start(), c)[1], 0)
    for copy in locals_:
        copy.wait()
    for count, make in copies:
        lax.fori_loop(1, count, lambda step, c, make=make: (make(step).wait(), c)[1], 0)


def collect_kernel(seqs, zeros, tok, cot, wgt, tok_out, cot_out, wgt_out, send, recv, wsend, wrecv, loc):
    me_s, me_z = lax.axis_index("seq"), lax.axis_index("zero")

    def along_seq(step):
        return (lax.rem(me_s + step, seqs), me_z)

    def along_zero(step):
        return (me_s, lax.rem(me_z + step, zeros))

    def token_copy(step):
        return pltpu.make_async_remote_copy(
            tok, tok_out.at[me_s], send.at[0, step], recv.at[0, step], along_seq(step), MESH
        )

    def cot_copy(step):
        target = along_seq(step)
        return pltpu.make_async_remote_copy(
            cot.at[target[0]], cot_out.at[me_s], send.at[1, step], recv.at[1, step], target, MESH
        )

    def weight_copy(step):
        return pltpu.make_async_remote_copy(
            wgt, wgt_out.at[me_z], wsend.at[step], wrecv.at[step], along_zero(step), MESH
        )

    greet(((seqs, along_seq), (zeros, along_zero)))
    run_copies(
        ((zeros, weight_copy), (seqs, token_copy), (seqs, cot_copy)),
        (
            pltpu.make_async_copy(tok, tok_out.at[me_s], loc.at[0]),
            pltpu.make_async_copy(cot.at[me_s], cot_out.at[me_s], loc.at[1]),
            pltpu.make_async_copy(wgt, wgt_out.at[me_z], loc.at[2]),
        ),
    )


def collect(tok, cot, wgt, seqs, zeros):
    anywhere = pl.BlockSpec(memory_space=pl.ANY)
    return pl.pallas_call(
        functools.partial(collect_kernel, seqs, zeros),
        out_shape=(
            jax.ShapeDtypeStruct((seqs,) + tok.shape, tok.dtype),
            jax.ShapeDtypeStruct(cot.shape, cot.dtype),
            jax.ShapeDtypeStruct((zeros,) + wgt.shape, wgt.dtype),
        ),
        in_specs=[anywhere] * 3,
        out_specs=(anywhere,) * 3,
        scratch_shapes=[
            pltpu.SemaphoreType.DMA((2, seqs)),
            pltpu.SemaphoreType.DMA((2, seqs)),
            pltpu.SemaphoreType.DMA((zeros,)),
            pltpu.SemaphoreType.DMA((zeros,)),
            pltpu.SemaphoreType.DMA((3,)),
        ],
        compiler_params=pltpu.CompilerParams(collective_id=0, has_side_effects=True),
        name="collect",
    )(tok, cot, wgt)


def deliver_kernel(seqs, zeros, tok, wgt, head, tok_out, wgt_out, head_out, tsend, trecv, send, recv, loc):
    me_s, me_z = lax.axis_index("seq"), lax.axis_index("zero")
    every = seqs * zeros
    me = me_s * zeros + me_z

    def along_seq(step):
        return (lax.rem(me_s + step, seqs), me_z)

    def anyone(step):
        target = lax.rem(me + step, every)
        return (target // zeros, lax.rem(target, zeros))

    def token_copy(step):
        target = along_seq(step)
        return pltpu.make_async_remote_copy(
            tok.at[target[0]], tok_out.at[me_s], tsend.at[step], trecv.at[step], target, MESH
        )

    def weight_copy(step):
        target = lax.rem(me + step, every)
        return pltpu.make_async_remote_copy(
            wgt.at[target], wgt_out.at[me], send.at[0, step], recv.at[0, step], anyone(step), MESH
        )

    def head_copy(step):
        return pltpu.make_async_remote_copy(
            head, head_out.at[me], send.at[1, step], recv.at[1, step], anyone(step), MESH
        )

    greet(((every, anyone),))
    run_copies(
        ((seqs, token_copy), (every, weight_copy), (every, head_copy)),
        (
            pltpu.make_async_copy(tok.at[me_s], tok_out.at[me_s], loc.at[0]),
            pltpu.make_async_copy(wgt.at[me], wgt_out.at[me], loc.at[1]),
            pltpu.make_async_copy(head, head_out.at[me], loc.at[2]),
        ),
    )


def deliver(tok, wgt, head, seqs, zeros):
    anywhere = pl.BlockSpec(memory_space=pl.ANY)
    every = seqs * zeros
    return pl.pallas_call(
        functools.partial(deliver_kernel, seqs, zeros),
        out_shape=(
            jax.ShapeDtypeStruct(tok.shape, tok.dtype),
            jax.ShapeDtypeStruct(wgt.shape, wgt.dtype),
            jax.ShapeDtypeStruct((every,) + head.shape, head.dtype),
        ),
        in_specs=[anywhere] * 3,
        out_specs=(anywhere,) * 3,
        scratch_shapes=[
            pltpu.SemaphoreType.DMA((seqs,)),
            pltpu.SemaphoreType.DMA((seqs,)),
            pltpu.SemaphoreType.DMA((2, every)),
            pltpu.SemaphoreType.DMA((2, every)),
            pltpu.SemaphoreType.DMA((3,)),
        ],
        compiler_params=pltpu.CompilerParams(collective_id=1, has_side_effects=True),
        name="deliver",
    )(tok, wgt, head)


def mixer_kernel(hp, pre_ref, dy_ref, par_ref, g_ref, head_ref, states, grad, acc):
    chunks, inner, group = dy_ref.shape
    top = inner + 2 * STATE
    slots = acc.shape[1]
    bias = par_ref[0][:, :1]
    rate = -jnp.exp(par_ref[1][:, :1])
    gain = par_ref[2][:, :1]
    row = lax.broadcasted_iota(jnp.int32, (group, group), 0)
    col = lax.broadcasted_iota(jnp.int32, (group, group), 1)
    causal = col >= row
    before = causal.astype(F32)
    after = (col <= row).astype(F32)

    def spread(rows):
        return jnp.concatenate(
            [jnp.broadcast_to(rows[h : h + 1], (HEAD_DIM, rows.shape[1])) for h in range(hp)], axis=0
        )

    def gather_rows(full):
        parts = [
            jnp.sum(full[h * HEAD_DIM : (h + 1) * HEAD_DIM], axis=0, keepdims=True) for h in range(hp)
        ]
        if slots > hp:
            parts.append(jnp.zeros((slots - hp, full.shape[1]), F32))
        return jnp.concatenate(parts, axis=0)

    def load(k):
        at = pl.ds(pl.multiple_of(k * group, group), group)
        pre = pre_ref[:inner, at]
        sig = jax.nn.sigmoid(pre)
        maps = pre_ref[inner:top, at]
        map_sig = jax.nn.sigmoid(maps)
        raw = pre_ref[top : top + slots, at] + bias
        step = jax.nn.softplus(raw)
        cum = exact(rate * step, before)
        return at, pre, sig, maps, map_sig, raw, step, cum

    grad[...] = jnp.zeros_like(grad)

    def forward(k, carry):
        at, pre, sig, maps, map_sig, raw, step, cum = load(k)
        last = cum[:, group - 1 :]
        x = pre * sig
        in_map = (maps[:STATE] * map_sig[:STATE]).astype(BF16)
        tail = (x * spread(step * jnp.exp(last - cum))).astype(BF16)
        held = grad[...]
        states[k] = held
        grad[...] = spread(jnp.exp(jnp.broadcast_to(last, (slots, STATE)))) * held + nt(tail, in_map)
        return carry

    lax.fori_loop(0, chunks, forward, 0)
    grad[...] = jnp.zeros_like(grad)
    acc[...] = jnp.zeros_like(acc)

    def backward(i, carry):
        k = chunks - 1 - i
        at, pre, sig, maps, map_sig, raw, step, cum = load(k)
        last = cum[:, group - 1 :]
        x = pre * sig
        both = maps * map_sig
        in_map = both[:STATE].astype(BF16)
        out_map = both[STATE:].astype(BF16)
        dy16 = dy_ref[k]
        dy = dy16.astype(F32)
        u = x * spread(step)
        u16 = u.astype(BF16)
        tail = spread(jnp.exp(last - cum))
        lead = spread(jnp.exp(cum))
        leave = spread(jnp.exp(jnp.broadcast_to(last, (slots, STATE))))
        held = states[k]
        held16 = held.astype(BF16)
        g_out = grad[...]
        g16 = g_out.astype(BF16)
        u_tail16 = (u * tail).astype(BF16)
        dy_lead = dy * lead
        dy_lead16 = dy_lead.astype(BF16)

        score = tn(in_map, out_map)
        cum_col = jnp.concatenate([cum, jnp.zeros((group - slots, group), F32)], axis=0).T
        d_score = jnp.zeros((group, group), F32)
        ksum = jnp.zeros((group, group), F32)
        du_parts = []
        r_parts = []
        for h in range(hp):
            at_h = slice(h * HEAD_DIM, (h + 1) * HEAD_DIM)
            diff = cum[h : h + 1] - cum_col[:, h : h + 1]
            within = jnp.where(causal, jnp.exp(jnp.where(causal, diff, 0.0)), 0.0)
            mixing = score * within
            d_mix = tn(u16[at_h], dy16[at_h])
            du_parts.append(nt(dy16[at_h], mixing.astype(BF16)))
            d_score = d_score + d_mix * within
            pair = d_mix * mixing
            r_parts.append(jnp.sum(pair, axis=0, keepdims=True))
            ksum = jnp.where(col == h, jnp.sum(pair, axis=1, keepdims=True), ksum)
        if slots > hp:
            r_parts.append(jnp.zeros((slots - hp, group), F32))
        from_tail = nn(g16, in_map) * tail
        tail_rows = gather_rows(u * from_tail)
        lead_rows = gather_rows(dy_lead * nn(held16, out_map))
        du = jnp.concatenate(du_parts, axis=0) + from_tail
        d_cum = jnp.concatenate(r_parts, axis=0) - ksum.T[:slots] + lead_rows - tail_rows
        cross = jnp.sum(gather_rows(held * g_out * leave) + tail_rows, axis=1, keepdims=True)
        d_log = exact(d_cum, after) + cross
        d_step = gather_rows(du * x) + rate * d_log
        d_raw = d_step * jax.nn.sigmoid(raw)

        d_score16 = d_score.astype(BF16)
        d_out = nn(in_map, d_score16) + tn(held16, dy_lead16)
        d_in = nt(out_map, d_score16) + tn(g16, u_tail16)
        grad[...] = leave * g_out + nt(dy_lead16, out_map)

        slope = sig * (1.0 + pre * (1.0 - sig))
        map_slope = map_sig * (1.0 + maps * (1.0 - map_sig))
        g_ref[:inner, at] = ((du * spread(step) + dy * gain_full) * slope).astype(BF16)
        g_ref[inner:top, at] = (jnp.concatenate([d_in, d_out], axis=0) * map_slope).astype(BF16)
        rest = g_ref.shape[0] - top
        g_ref[top:, at] = jnp.concatenate(
            [d_raw, jnp.zeros((rest - slots, group), F32)], axis=0
        ).astype(BF16)
        acc[0] += d_raw
        acc[1] += d_log * (rate * step)
        acc[2] += gather_rows(dy * x)
        return carry

    gain_full = spread(jnp.broadcast_to(gain, (slots, group)))
    lax.fori_loop(0, chunks, backward, 0)
    for i in range(3):
        head_ref[i] = jnp.broadcast_to(jnp.sum(acc[i], axis=1, keepdims=True), head_ref.shape[1:])


def mixer(pre, dy, par, hp):
    chunks, inner, group = dy.shape
    slots = par.shape[1]
    return pl.pallas_call(
        functools.partial(mixer_kernel, hp),
        out_shape=(
            jax.ShapeDtypeStruct(pre.shape, BF16),
            jax.ShapeDtypeStruct((3, slots, 128), F32),
        ),
        in_specs=[pl.BlockSpec(memory_space=pltpu.VMEM)] * 3,
        out_specs=(pl.BlockSpec(memory_space=pltpu.VMEM),) * 2,
        scratch_shapes=[
            pltpu.VMEM((chunks, inner, STATE), F32),
            pltpu.VMEM((inner, STATE), F32),
            pltpu.VMEM((3, slots, group), F32),
        ],
        compiler_params=pltpu.CompilerParams(vmem_limit_bytes=48 * 1024 * 1024),
        name="mixer",
    )(pre, dy, par)


def body(seqs, zeros, hidden, output_grad, input_weight, step_bias, decay_log, skip_gain):
    heads = step_bias.shape[0]
    hp = up(heads, seqs) // seqs
    slots = up(hp, 8)
    inner, full = hp * HEAD_DIM, heads * HEAD_DIM
    spare = seqs * hp - heads
    width = up(inner + 2 * STATE + slots, 128)
    me = lax.axis_index("seq")
    length, model = hidden.shape[1:]

    def own(array, axis, size, extra):
        if extra:
            pads = [(0, 0)] * array.ndim
            pads[axis] = (0, extra)
            array = jnp.pad(array, pads)
        return lax.dynamic_slice_in_dim(array, me * size, size, axis)

    weight = jnp.concatenate(
        [
            own(input_weight[:, :full], 1, inner, spare * HEAD_DIM),
            input_weight[:, full : full + 2 * STATE],
            own(input_weight[:, full + 2 * STATE :], 1, hp, spare),
            jnp.zeros((input_weight.shape[0], width - inner - 2 * STATE - hp), BF16),
        ],
        axis=1,
    )
    cot = jnp.pad(output_grad[0], ((0, 0), (0, spare * HEAD_DIM))).T.reshape(seqs, inner, length)
    par = jnp.stack([own(v, 0, hp, spare) for v in (step_bias, decay_log, skip_gain)])
    par = jnp.broadcast_to(jnp.pad(par, ((0, 0), (0, slots - hp)))[:, :, None], (3, slots, 128))

    tokens, dy, columns = collect(hidden[0], cot, weight, seqs, zeros)
    tokens = tokens.reshape(seqs * length, model)
    columns = columns.reshape(model, width)
    pre = lax.dot_general(columns, tokens, (((0,), (1,)), ((), ())), preferred_element_type=F32)
    grads, sums = mixer(pre, dy, par, hp)
    token_part = tn(grads, columns_t(columns)).astype(BF16).reshape(seqs, length, model)
    weight_part = lax.dot_general(
        tokens, grads, (((0,), (1,)), ((), ())), preferred_element_type=F32
    ).astype(BF16)
    every = seqs * zeros
    weight_part = weight_part.reshape(every, model // every, width)

    token_all, weight_all, sums_all = deliver(token_part, weight_part, sums, seqs, zeros)
    token_grad = jnp.sum(token_all.astype(F32), axis=0).astype(BF16)
    rows = jnp.sum(
        weight_all.reshape(seqs, zeros, model // every, width).astype(F32), axis=1
    )
    parts = rows.transpose(1, 0, 2)
    weight_grad = jnp.concatenate(
        [
            parts[:, :, :inner].reshape(-1, seqs * inner)[:, :full],
            jnp.sum(rows[:, :, inner : inner + 2 * STATE], axis=0),
            parts[:, :, inner + 2 * STATE : inner + 2 * STATE + hp].reshape(-1, seqs * hp)[:, :heads],
        ],
        axis=1,
    )
    sums_all = jnp.sum(sums_all.reshape(seqs, zeros, 3, slots, 128)[:, :, :, :hp, 0], axis=1)
    head_grads = sums_all.transpose(1, 0, 2).reshape(3, seqs * hp)[:, :heads]
    return (token_grad[None], weight_grad, head_grads)


def columns_t(columns):
    return columns.T


def solution(mesh):
    placed = (P("zero", "seq", None), P("zero", "seq", None), P("zero", None), P(), P(), P())
    return jax.shard_map(
        functools.partial(body, mesh.shape["seq"], mesh.shape["zero"]),
        mesh=mesh,
        in_specs=placed,
        out_specs=(P("zero", "seq", None), P(("seq", "zero"), None), P()),
        check_vma=False,
    )
```

time: 588 us -> 141 us (0.24)
  waiting for transfers between devices: 417 us -> 0 us
  Pallas kernels: 0 us -> 114 us
  blocking collectives: 54.4 us -> 0 us
  matrix products: 46.5 us -> 11.5 us
  local copies, waits for them, and re-layouts: 29.6 us -> 7.59 us
  other arithmetic: 19.6 us -> 5.3 us
  between operations: 14.8 us -> 0.79 us
    all_gather x3 -> x0, waiting for transfers between devices: 240 us -> none  [the longest x1 135 us: body(): lax.all_gather(input_weight, 'zero', axis=0, tiled=True)]
    unnamed x7 -> x0, waiting for transfers between devices: 177 us -> none
    pallas_call x0 -> x3, Pallas kernels: none -> 114 us  [the longest x1 59.8 us: deliver(): pl.pallas_call(functools.partial(deliver_kernel, seqs, zeros), out_shape=...]
    psum x1 -> x0, blocking collectives: 45 us -> none  [body(): lax.psum(jnp.stack([bias_grad, log_grad, gain_grad]), ('seq', 'zero'))]
    dot_general x14 -> x3, matrix products: 46.5 us -> 11.5 us  [the longest x1 4.21 us: body(): lax.dot_general(columns, tokens, (((0,), (1,)), ((), ())), preferred_elem...]
    unnamed x38 -> x14, local copies, waits for them, and re-layouts: 28.4 us -> 0.67 us
    add x7 -> x0, other arithmetic: 11 us -> none  [combine_states(): jnp.exp(later[0])[:, None, None] * earlier[1] + later[1]]
    all_gather x1 -> x0, blocking collectives: 9.44 us -> none  [prefix(): gathered = jax.tree.map(lambda a: lax.all_gather(a, axis), part)]
  transfers between devices with their start and end apart: 5 -> 0, of which waited for: 5 -> 0; matrix products, arithmetic and copies ran while one was open for 4% -> 0% of each run, Pallas kernels for 0% -> 0%
where the time goes in v1:
time: 141 us; the launch traced here: 139 us
  Pallas kernels  114 us (81%)
  matrix products  11.5 us (8%)
  local copies, waits for them, and re-layouts  7.59 us (5%)
  other arithmetic  5.3 us (4%)
    pallas_call x1, Pallas kernels, deliver(): pl.pallas_call(functools.partial(deliver_kernel, seqs, zeros), out_shape=...  59.8 us
    pallas_call x1, Pallas kernels, collect(): pl.pallas_call(functools.partial(collect_kernel, seqs, zeros), out_shape=...  40.7 us
    pallas_call x1, Pallas kernels, mixer(): pl.pallas_call(functools.partial(mixer_kernel, hp), out_shape=(jax.ShapeD...  13.9 us
    dot_general x1, matrix products, body(): lax.dot_general(columns, tokens, (((0,), (1,)), ((), ())), preferred_elem...  4.21 us
    dot_general x1, matrix products, tn(): lax.dot_general(a, b, (((0,), (0,)), ((), ())), preferred_element_type=F32)  3.77 us
    dot_general x1, matrix products, body(): lax.dot_general(tokens, grads, (((0,), (1,)), ((), ())), preferred_elemen...  3.5 us
    reduce_sum x1, other arithmetic, body(): token_grad = jnp.sum(token_all.astype(F32), axis=0).astype(BF16)  3.05 us

profile of v1, /device:TPU:9, one launch (start us, length us, event | category | flops | bytes accessed | tf_op | source)
XLA Modules:
  0.0 139.5 jit_solution(994634029032660646)
XLA Ops:
  0.6 0.0 copy-start
  0.7 0.6 copy-done
  1.3 0.1 dynamic-slice_bitcast_fusion.2
  1.4 0.7 dynamic-slice_bitcast_fusion
  2.1 0.1 pad.14.clone
  2.2 0.1 broadcast_in_dim.13.par_ref
  2.3 0.9 slice.23
  3.2 0.1 constant_dynamic-slice_fusion
  3.3 2.2 %copy.19 = bf16[2560,128]{1,0:T(8,128)(2,1)} copy(bf16[2560,128]{0,1:T(8,128)(2,1)} %bitcast.35) | data formatting | bytes 1310720 | tf_op jit(solution)/shard_map/transpose | solution.py:364
  5.4 0.0 slice-start.1
  5.4 0.0 slice-start
  5.4 1.4 %slice-done.1 = bf16[320,2560]{1,0:T(8,128)(2,1)S(1)} async-done(((bf16[320,2856]{1,0:T(8,128)(2,1)}), bf16[320,2560]{1,0:T(8,128)(2,1)S(1)}, s32[]{:S(2)}) %slice-start.1) | async-done | bytes 1638424 | tf_op jit(solution)/shard_map/slice | solution.py:357
  6.9 0.1 constant_dynamic-slice_fusion.1
  7.0 0.0 slice-done
  7.0 0.9 maximum_maximum_fusion.wgt
  8.0 40.7 %collect.1 = (bf16[8,128,1280]{2,1,0:T(8,128)(2,1)}, bf16[8,320,128]{2,1,0:T(8,128)(2,1)}, bf16[4,320,640]{2,1,0:T(8,128)(2,1)}) custom-call(bf16[128,1280]{1,0:T(8,128)(2,1)} %bitcast.38, bf16[8,320,128]{2,1,0:T(8,128)(2,1)} %bitcast.33, bf16[320,640]{1,0:T(8,128)(2,1)} %maximum_maximum_fusion.wgt), custom_call_target="tpu_custom_call" | custom-call | tf_op jit(solution)/shard_map/collect/pallas_call | solution.py:102
  48.6 0.0 copy-start.1
  48.7 4.2 %fusion.pre_ref = f32[640,1024]{1,0:T(8,128)S(1)} fusion(bf16[1280,640]{1,0:T(8,128)(2,1)} %bitcast.42, bf16[1024,1280]{1,0:T(8,128)(2,1)} %bitcast.40), kind=kOutput, calls=%fused_computation.15 | convolution fusion | flops 1677721600 | bytes 6881280 | tf_op jit(solution)/shard_map/dot_general | solution.py:371
  52.9 0.0 copy-done.1
  52.9 0.0 copy-start.5
  52.9 13.9 %mixer.1 = (bf16[640,1024]{1,0:T(8,128)(2,1)S(1)}, f32[3,8,128]{2,1,0:T(8,128)S(1)}) custom-call(f32[640,1024]{1,0:T(8,128)S(1)} %fusion.pre_ref, bf16[8,320,128]{2,1,0:T(8,128)(2,1)S(1)} %copy-done.1, f32[3,8,128]{2,1,0:T(8,128)S(1)} %broadcast_in_dim.13.par_ref), custom_call_target="tpu_custom_call" | custom-call | tf_op jit(solution)/shard_map/mixer/pallas_call | solution.py:320
  66.8 0.0 copy-start.2
  66.8 0.0 copy-done.5
  66.8 0.0 copy-start.6
  66.8 3.5 %convolution_convert_fusion.1 = bf16[1280,640]{1,0:T(8,128)(2,1)} fusion(bf16[1024,1280]{1,0:T(8,128)(2,1)S(1)} %bitcast.41, bf16[640,1024]{1,0:T(8,128)(2,1)S(1)} %get-tuple-element.14), kind=kOutput, calls=%fused_computation.2 | convolution fusion | flops 1678540800 | bytes 5570560 | tf_op jit(solution)/shard_map/dot_general | solution.py:374
  70.3 0.0 copy-done.2
  70.3 0.0 copy-done.6
  70.3 3.8 %convolution_convert_fusion = bf16[1024,1280]{1,0:T(8,128)(2,1)} fusion(bf16[640,1024]{1,0:T(8,128)(2,1)S(1)} %get-tuple-element.14, bf16[1280,640]{1,0:T(8,128)(2,1)S(1)} %bitcast.43), kind=kOutput, calls=%fused_computation | convolution fusion | flops 1679032320 | bytes 5570560 | tf_op jit(solution)/shard_map/dot_general | solution.py:30
  74.1 59.8 %deliver.1 = (bf16[8,128,1280]{2,1,0:T(8,128)(2,1)}, bf16[32,40,640]{2,1,0:T(8,128)(2,1)}, f32[32,3,8,128]{3,2,1,0:T(8,128)}) custom-call(bf16[8,128,1280]{2,1,0:T(8,128)(2,1)} %bitcast.32, bf16[32,40,640]{2,1,0:T(8,128)(2,1)} %bitcast.34, f32[3,8,128]{2,1,0:T(8,128)} %copy-done.2), custom_call_target="tpu_custom_call" | custom-call | tf_op jit(solution)/shard_map/deliver/pallas_call | solution.py:166
  133.8 0.0 copy-start.4
  133.8 0.0 copy-start.3
  133.8 3.0 %reduce_sum.39 = bf16[128,1280]{1,0:T(8,128)(2,1)} reduce(bf16[8,128,1280]{2,1,0:T(8,128)(2,1)} %get-tuple-element.16, bf16[]{:T(256)} %constant.20.clone.1), dimensions={0}, to_apply=%region_0.1 | reduce | flops 1146880 | bytes 2949122 | tf_op jit(solution)/shard_map/reduce_sum | solution.py:381
  136.9 0.0 copy-done.4
  136.9 0.1 slice_reduce_fusion
  137.0 0.7 reshape.45
  137.7 0.0 copy-done.3
  137.7 0.2 convert_reduce_fusion
  137.9 0.1 slice_reduce_fusion.1
  138.1 0.1 slice.30
  138.2 0.1 copy.22
  138.4 0.1 copy.24
  138.4 0.1 copy.20
  138.6 0.1 reshape.42
  138.7 0.8 pad_maximum_fusion
  (5 shorter events, 0.1 us)
Async XLA Ops:
  0.6 0.7 copy-start
  5.4 1.4 %slice-start.1 = ((bf16[320,2856]{1,0:T(8,128)(2,1)}), bf16[320,2560]{1,0:T(8,128)(2,1)S(1)}, s32[]{:S(2)}) async-start(bf16[320,2856]{1,0:T(8,128)(2,1)} %param.8), calls=%async_computation.1 | async-start | bytes 3276800 | tf_op jit(solution)/shard_map/slice | solution.py:357
  5.4 1.6 %slice-start = ((bf16[320,2856]{1,0:T(8,128)(2,1)}), bf16[320,256]{1,0:T(8,128)(2,1)S(1)}, s32[]{:S(2)}) async-start(bf16[320,2856]{1,0:T(8,128)(2,1)} %param.8), calls=%async_computation | async-start | bytes 327680 | tf_op jit(solution)/shard_map/slice | solution.py:358
  48.6 4.2 %copy-start.1 = (bf16[8,320,128]{2,1,0:T(8,128)(2,1)S(1)}, bf16[8,320,128]{2,1,0:T(8,128)(2,1)}, u32[]{:S(2)}) copy-start(bf16[8,320,128]{2,1,0:T(8,128)(2,1)} %get-tuple-element.13.dy_ref) | copy-start | bytes 1966084
  52.9 13.9 %copy-start.5 = (bf16[8,128,1280]{2,1,0:T(8,128)(2,1)S(1)}, bf16[8,128,1280]{2,1,0:T(8,128)(2,1)}, u32[]{:S(2)}) copy-start(bf16[8,128,1280]{2,1,0:T(8,128)(2,1)} %get-tuple-element.12) | copy-start | bytes 7864324
  66.8 3.5 %copy-start.2 = (f32[3,8,128]{2,1,0:T(8,128)}, f32[3,8,128]{2,1,0:T(8,128)S(1)}, u32[]{:S(2)}) copy-start(f32[3,8,128]{2,1,0:T(8,128)S(1)} %get-tuple-element.15.head) | copy-start | bytes 36868
  66.8 3.5 %copy-start.6 = (bf16[4,320,640]{2,1,0:T(8,128)(2,1)S(1)}, bf16[4,320,640]{2,1,0:T(8,128)(2,1)}, u32[]{:S(2)}) copy-start(bf16[4,320,640]{2,1,0:T(8,128)(2,1)} %get-tuple-element.11) | copy-start | bytes 4915204
  133.8 3.1 %copy-start.4 = (f32[32,3,8,128]{3,2,1,0:T(8,128)S(1)}, f32[32,3,8,128]{3,2,1,0:T(8,128)}, u32[]{:S(2)}) copy-start(f32[32,3,8,128]{3,2,1,0:T(8,128)} %get-tuple-element.18) | copy-start | bytes 1179652
  133.8 3.9 %copy-start.3 = (bf16[32,40,640]{2,1,0:T(8,128)(2,1)S(1)}, bf16[32,40,640]{2,1,0:T(8,128)(2,1)}, u32[]{:S(2)}) copy-start(bf16[32,40,640]{2,1,0:T(8,128)(2,1)} %get-tuple-element.17) | copy-start | bytes 4915204

commit v2 on v1

v2 whole, which is shorter than its diff:
```python
import functools

import jax
import jax.numpy as jnp
from jax import lax
from jax.experimental import pallas as pl
from jax.experimental.pallas import tpu as pltpu
from jax.sharding import PartitionSpec as P

HEAD_DIM = 64
STATE = 128
MESH = pl.DeviceIdType.MESH
F32 = jnp.float32
BF16 = jnp.bfloat16


def up(size, unit):
    return -(-size // unit) * unit


def nn(a, b):
    return lax.dot_general(a, b, (((1,), (0,)), ((), ())), preferred_element_type=F32)


def nt(a, b):
    return lax.dot_general(a, b, (((1,), (1,)), ((), ())), preferred_element_type=F32)


def tn(a, b):
    return lax.dot_general(a, b, (((0,), (0,)), ((), ())), preferred_element_type=F32)


def halves(a):
    high = a.astype(BF16)
    return high, (a - high.astype(F32)).astype(BF16)


def fine(dot, a, b):
    if a.dtype == BF16:
        high, low = halves(b)
        return dot(a, high) + dot(a, low)
    if b.dtype == BF16:
        high, low = halves(a)
        return dot(high, b) + dot(low, b)
    (ah, al), (bh, bl) = halves(a), halves(b)
    return dot(ah, bh) + (dot(al, bh) + dot(ah, bl))


def exact(a, b):
    return lax.dot_general(
        a, b, (((1,), (0,)), ((), ())), precision=lax.Precision.HIGHEST, preferred_element_type=F32
    )


def greet(peers):
    barrier = pltpu.get_barrier_semaphore()
    for peer in peers:
        pl.semaphore_signal(barrier, inc=1, device_id=peer, device_id_type=MESH)
    pl.semaphore_wait(barrier, len(peers))


def remote(src, dst, send, recv, peer):
    return pltpu.make_async_remote_copy(src, dst, send, recv, peer, MESH)


def collect_kernel(
    seqs, zeros, tok, cot, wgt, tok_out, cot_out, wgt_out, wsib_out,
    tsem, fsem, csem, rsem, ssem, loc,
):
    me_s, me_z = lax.axis_index("seq"), lax.axis_index("zero")
    chips = seqs // 2
    chip, core = me_s // 2, lax.rem(me_s, 2)
    sibling = (chip * 2 + 1 - core, me_z)
    half = wgt.shape[0] // 2
    full_hops = (zeros - 1) // 2
    upper, lower = pl.ds(0, half), pl.ds(half, wgt.shape[0] - half)

    def along(step):
        return (lax.rem(me_s + step, seqs), me_z)

    def owner(shift):
        return lax.rem(me_z + shift + zeros, zeros)

    right, left = (me_s, owner(1)), (me_s, owner(-1))
    greet([along(i) for i in range(1, seqs)] + ([right, left] if zeros > 1 else []))

    own = [
        pltpu.make_async_copy(tok, tok_out.at[me_s], loc.at[0]),
        pltpu.make_async_copy(cot.at[me_s], cot_out.at[me_s], loc.at[1]),
        pltpu.make_async_copy(wgt, wgt_out.at[me_z], loc.at[2]),
    ]

    def hop(way, h):
        at = owner(-way * (h - 1))
        src = wgt if h == 1 else wgt_out.at[at]
        dst = wgt_out.at[at]
        if h > full_hops:
            rows = upper if way > 0 else lower
            src, dst = src.at[rows], dst.at[rows]
        row = 0 if way > 0 else 2
        return remote(src, dst, rsem.at[row, h], rsem.at[row + 1, h], right if way > 0 else left)

    hops = full_hops + (1 - zeros % 2)
    ring = [(hop(1, h), hop(-1, h)) for h in range(1, hops + 1)]

    def token_slot(step):
        return lax.rem(chip - step + chips, chips) * 2 + core

    tokens = [
        remote(
            tok, tok_out.at[me_s], tsem.at[0, d], tsem.at[1, d],
            (lax.rem(chip + d, chips) * 2 + core, me_z),
        )
        for d in range(1, chips)
    ]
    cots = []
    for d in range(1, seqs):
        peer = along(d)
        cots.append(
            remote(cot.at[peer[0]], cot_out.at[me_s], csem.at[0, d], csem.at[1, d], peer)
        )
    passed = [remote(tok, tok_out.at[me_s], fsem.at[0, 0], fsem.at[1, 0], sibling)]
    for d in range(1, chips):
        at = token_slot(d)
        passed.append(remote(tok_out.at[at], tok_out.at[at], fsem.at[0, d], fsem.at[1, d], sibling))

    def share(slot, at, src):
        return remote(src, wsib_out.at[at], ssem.at[0, slot], ssem.at[1, slot], sibling)

    shared = [share(0, me_z, wgt)]
    for d in range(1, zeros):
        at = owner(-d)
        shared.append(share(d, at, wgt_out.at[at]))

    for copy in ring[0] if ring else ():
        copy.start()
    for copy in tokens + cots + [passed[0], shared[0]] + own:
        copy.start()
    for h in range(1, hops):
        for way in (0, 1):
            ring[h - 1][way].wait_recv()
            ring[h][way].start()
    for d in range(1, chips):
        tokens[d - 1].wait_recv()
        passed[d].start()
    if ring:
        for way in (0, 1):
            ring[-1][way].wait_recv()
    for copy in shared[1:]:
        copy.start()
    for pair in ring:
        for copy in pair:
            copy.wait_send()
    for copy in tokens:
        copy.wait_send()
    for copy in own + cots + passed + shared:
        copy.wait()


def collect(tok, cot, wgt, seqs, zeros):
    anywhere = pl.BlockSpec(memory_space=pl.ANY)
    columns = jax.ShapeDtypeStruct((zeros,) + wgt.shape, wgt.dtype)
    return pl.pallas_call(
        functools.partial(collect_kernel, seqs, zeros),
        out_shape=(
            jax.ShapeDtypeStruct((seqs,) + tok.shape, tok.dtype),
            jax.ShapeDtypeStruct(cot.shape, cot.dtype),
            columns,
            columns,
        ),
        in_specs=[anywhere] * 3,
        out_specs=(anywhere,) * 4,
        scratch_shapes=[
            pltpu.SemaphoreType.DMA((2, seqs)),
            pltpu.SemaphoreType.DMA((2, seqs)),
            pltpu.SemaphoreType.DMA((2, seqs)),
            pltpu.SemaphoreType.DMA((4, zeros + 1)),
            pltpu.SemaphoreType.DMA((2, zeros)),
            pltpu.SemaphoreType.DMA((3,)),
        ],
        compiler_params=pltpu.CompilerParams(collective_id=0, has_side_effects=True),
        name="collect",
    )(tok, cot, wgt)


def swap_kernel(give, got, send, recv):
    me_s, me_z = lax.axis_index("seq"), lax.axis_index("zero")
    sibling = (me_s // 2 * 2 + 1 - lax.rem(me_s, 2), me_z)
    greet([sibling])
    copy = remote(give.at[1], got, send, recv, sibling)
    copy.start()
    copy.wait()


def swap(split):
    return pl.pallas_call(
        swap_kernel,
        out_shape=jax.ShapeDtypeStruct(split.shape[1:], split.dtype),
        in_specs=[pl.BlockSpec(memory_space=pltpu.VMEM)],
        out_specs=pl.BlockSpec(memory_space=pltpu.VMEM),
        scratch_shapes=[pltpu.SemaphoreType.DMA, pltpu.SemaphoreType.DMA],
        compiler_params=pltpu.CompilerParams(collective_id=2, has_side_effects=True),
        name="swap",
    )(split)


def deliver_kernel(
    seqs, zeros, tok, wgt, head, tok_out, wgt_out, head_out,
    zin, zsum, tsem, zsem, wsem, hsem, loc,
):
    me_s, me_z = lax.axis_index("seq"), lax.axis_index("zero")
    every = seqs * zeros
    me = me_s * zeros + me_z
    chips = seqs // 2
    chip, core = me_s // 2, lax.rem(me_s, 2)

    def anyone(step):
        target = lax.rem(me + step, every)
        return (target // zeros, lax.rem(target, zeros))

    barrier = pltpu.get_barrier_semaphore()

    def signal(step, carry):
        pl.semaphore_signal(barrier, inc=1, device_id=anyone(step), device_id_type=MESH)
        return carry

    lax.fori_loop(1, every, signal, 0)
    pl.semaphore_wait(barrier, every - 1)

    def head_copy(step):
        return remote(head, head_out.at[me], hsem.at[0, step], hsem.at[1, step], anyone(step))

    across = []
    for d in range(1, zeros):
        target = lax.rem(me_z + d, zeros)
        across.append(
            remote(wgt.at[:, target], zin.at[d], zsem.at[0, d], zsem.at[1, d], (me_s, target))
        )
    tokens = []
    for d in range(1, chips):
        target = lax.rem(chip + d, chips)
        tokens.append(
            remote(
                tok.at[target], tok_out.at[chip], tsem.at[0, d], tsem.at[1, d],
                (target * 2 + core, me_z),
            )
        )
    own = [
        pltpu.make_async_copy(tok.at[chip], tok_out.at[chip], loc.at[0]),
        pltpu.make_async_copy(head, head_out.at[me], loc.at[1]),
    ]
    first = pltpu.make_async_copy(wgt.at[:, me_z], zin.at[0], loc.at[2])
    first.start()
    for copy in across + tokens + own:
        copy.start()
    lax.fori_loop(1, every, lambda i, c: (head_copy(i).start(), c)[1], 0)
    first.wait()
    for copy in across:
        copy.wait()

    def add(j, carry):
        total = zin[0, j].astype(F32)
        for d in range(1, zeros):
            total = total + zin[d, j].astype(F32)
        zsum[j] = total.astype(BF16)
        return carry

    lax.fori_loop(0, seqs, add, 0)
    last = pltpu.make_async_copy(zsum.at[me_s], wgt_out.at[me_s], loc.at[3])
    last.start()
    along = []
    for d in range(1, seqs):
        target = lax.rem(me_s + d, seqs)
        along.append(
            remote(
                zsum.at[target], wgt_out.at[me_s], wsem.at[0, d], wsem.at[1, d], (target, me_z)
            )
        )
    for copy in along:
        copy.start()
    for copy in own + [last] + tokens + along:
        copy.wait()
    lax.fori_loop(1, every, lambda i, c: (head_copy(i).wait(), c)[1], 0)


def deliver(tok, wgt, head, seqs, zeros):
    anywhere = pl.BlockSpec(memory_space=pl.ANY)
    every = seqs * zeros
    block = wgt.shape[2:]
    return pl.pallas_call(
        functools.partial(deliver_kernel, seqs, zeros),
        out_shape=(
            jax.ShapeDtypeStruct(tok.shape, tok.dtype),
            jax.ShapeDtypeStruct((seqs,) + block, wgt.dtype),
            jax.ShapeDtypeStruct((every,) + head.shape, head.dtype),
        ),
        in_specs=[anywhere] * 3,
        out_specs=(anywhere,) * 3,
        scratch_shapes=[
            pltpu.VMEM((zeros, seqs) + block, BF16),
            pltpu.VMEM((seqs,) + block, BF16),
            pltpu.SemaphoreType.DMA((2, seqs)),
            pltpu.SemaphoreType.DMA((2, zeros)),
            pltpu.SemaphoreType.DMA((2, seqs)),
            pltpu.SemaphoreType.DMA((2, every)),
            pltpu.SemaphoreType.DMA((4,)),
        ],
        compiler_params=pltpu.CompilerParams(collective_id=1, has_side_effects=True),
        name="deliver",
    )(tok, wgt, head)


def mixer_kernel(hp, pre_ref, dy_ref, par_ref, g_ref, split_ref, head_ref, states, grad, acc):
    chunks, inner, group = dy_ref.shape
    top = inner + 2 * STATE
    slots = acc.shape[1]
    core = lax.rem(lax.axis_index("seq"), 2)
    bias = par_ref[0][:, :1]
    rate = -jnp.exp(par_ref[1][:, :1])
    gain = par_ref[2][:, :1]
    row = lax.broadcasted_iota(jnp.int32, (group, group), 0)
    col = lax.broadcasted_iota(jnp.int32, (group, group), 1)
    causal = col >= row
    before = causal.astype(F32)
    after = (col <= row).astype(F32)

    def spread(rows):
        return jnp.concatenate(
            [jnp.broadcast_to(rows[h : h + 1], (HEAD_DIM, rows.shape[1])) for h in range(hp)], axis=0
        )

    def gather_rows(full):
        parts = [
            jnp.sum(full[h * HEAD_DIM : (h + 1) * HEAD_DIM], axis=0, keepdims=True) for h in range(hp)
        ]
        if slots > hp:
            parts.append(jnp.zeros((slots - hp, full.shape[1]), F32))
        return jnp.concatenate(parts, axis=0)

    def load(k):
        at = pl.ds(pl.multiple_of(k * group, group), group)
        pre = pre_ref[:inner, at]
        sig = jax.nn.sigmoid(pre)
        maps = pre_ref[inner:top, at]
        map_sig = jax.nn.sigmoid(maps)
        raw = pre_ref[top : top + slots, at] + bias
        step = jax.nn.softplus(raw)
        cum = exact(rate * step, before)
        return at, pre, sig, maps, map_sig, raw, step, cum

    grad[...] = jnp.zeros_like(grad)

    def forward(k, carry):
        at, pre, sig, maps, map_sig, raw, step, cum = load(k)
        last = cum[:, group - 1 :]
        x = pre * sig
        in_map = maps[:STATE] * map_sig[:STATE]
        tail = x * spread(step * jnp.exp(last - cum))
        held = grad[...]
        states[k] = held
        grad[...] = spread(jnp.exp(jnp.broadcast_to(last, (slots, STATE)))) * held + fine(nt, tail, in_map)
        return carry

    lax.fori_loop(0, chunks, forward, 0)
    grad[...] = jnp.zeros_like(grad)
    acc[...] = jnp.zeros_like(acc)

    def backward(i, carry):
        k = chunks - 1 - i
        at, pre, sig, maps, map_sig, raw, step, cum = load(k)
        last = cum[:, group - 1 :]
        x = pre * sig
        both = maps * map_sig
        in_map = both[:STATE]
        out_map = both[STATE:]
        dy16 = dy_ref[k]
        dy = dy16.astype(F32)
        u = x * spread(step)
        tail = spread(jnp.exp(last - cum))
        lead = spread(jnp.exp(cum))
        leave = spread(jnp.exp(jnp.broadcast_to(last, (slots, STATE))))
        held = states[k]
        g_out = grad[...]
        u_tail = u * tail
        dy_lead = dy * lead

        score = fine(tn, in_map, out_map)
        cum_col = jnp.concatenate([cum, jnp.zeros((group - slots, group), F32)], axis=0).T
        d_score = jnp.zeros((group, group), F32)
        ksum = jnp.zeros((group, group), F32)
        du_parts = []
        r_parts = []
        for h in range(hp):
            at_h = slice(h * HEAD_DIM, (h + 1) * HEAD_DIM)
            diff = cum[h : h + 1] - cum_col[:, h : h + 1]
            within = jnp.where(causal, jnp.exp(jnp.where(causal, diff, 0.0)), 0.0)
            mixing = score * within
            d_mix = fine(tn, u[at_h], dy16[at_h])
            du_parts.append(fine(nt, dy16[at_h], mixing))
            d_score = d_score + d_mix * within
            pair = d_mix * mixing
            r_parts.append(jnp.sum(pair, axis=0, keepdims=True))
            ksum = jnp.where(col == h, jnp.sum(pair, axis=1, keepdims=True), ksum)
        if slots > hp:
            r_parts.append(jnp.zeros((slots - hp, group), F32))
        from_tail = fine(nn, g_out, in_map) * tail
        tail_rows = gather_rows(u * from_tail)
        lead_rows = gather_rows(dy_lead * fine(nn, held, out_map))
        du = jnp.concatenate(du_parts, axis=0) + from_tail
        d_cum = jnp.concatenate(r_parts, axis=0) - ksum.T[:slots] + lead_rows - tail_rows
        cross = jnp.sum(gather_rows(held * g_out * leave) + tail_rows, axis=1, keepdims=True)
        d_log = exact(d_cum, after) + cross
        d_step = gather_rows(du * x) + rate * d_log
        d_raw = d_step * jax.nn.sigmoid(raw)

        d_out = fine(nn, in_map, d_score) + fine(tn, held, dy_lead)
        d_in = fine(nt, out_map, d_score) + fine(tn, g_out, u_tail)
        grad[...] = leave * g_out + fine(nt, dy_lead, out_map)

        slope = sig * (1.0 + pre * (1.0 - sig))
        map_slope = map_sig * (1.0 + maps * (1.0 - map_sig))
        rest = g_ref.shape[0] - top - slots
        rounded = jnp.concatenate(
            [
                (du * spread(step) + dy * gain_full) * slope,
                jnp.concatenate([d_in, d_out], axis=0) * map_slope,
                d_raw,
                jnp.zeros((rest, group), F32),
            ],
            axis=0,
        ).astype(BF16)
        g_ref[:, at] = rounded
        split_ref[lax.rem(k + core, 2), k // 2] = rounded
        acc[0] += d_raw
        acc[1] += d_log * (rate * step)
        acc[2] += gather_rows(dy * x)
        return carry

    gain_full = spread(jnp.broadcast_to(gain, (slots, group)))
    lax.fori_loop(0, chunks, backward, 0)
    for i in range(3):
        head_ref[i] = jnp.broadcast_to(jnp.sum(acc[i], axis=1, keepdims=True), head_ref.shape[1:])


def mixer(pre, dy, par, hp):
    chunks, inner, group = dy.shape
    slots = par.shape[1]
    return pl.pallas_call(
        functools.partial(mixer_kernel, hp),
        out_shape=(
            jax.ShapeDtypeStruct(pre.shape, BF16),
            jax.ShapeDtypeStruct((2, chunks // 2, pre.shape[0], group), BF16),
            jax.ShapeDtypeStruct((3, slots, 128), F32),
        ),
        in_specs=[pl.BlockSpec(memory_space=pltpu.VMEM)] * 3,
        out_specs=(pl.BlockSpec(memory_space=pltpu.VMEM),) * 3,
        scratch_shapes=[
            pltpu.VMEM((chunks, inner, STATE), F32),
            pltpu.VMEM((inner, STATE), F32),
            pltpu.VMEM((3, slots, group), F32),
        ],
        compiler_params=pltpu.CompilerParams(vmem_limit_bytes=48 * 1024 * 1024),
        name="mixer",
    )(pre, dy, par)


def body(seqs, zeros, hidden, output_grad, input_weight, step_bias, decay_log, skip_gain):
    heads = step_bias.shape[0]
    hp = up(heads, seqs) // seqs
    slots = up(hp, 8)
    inner, full = hp * HEAD_DIM, heads * HEAD_DIM
    spare = seqs * hp - heads
    width = up(inner + 2 * STATE + slots, 128)
    me = lax.axis_index("seq")
    length, model = hidden.shape[1:]

    def own(array, axis, size, extra):
        if extra:
            pads = [(0, 0)] * array.ndim
            pads[axis] = (0, extra)
            array = jnp.pad(array, pads)
        return lax.dynamic_slice_in_dim(array, me * size, size, axis)

    weight = jnp.concatenate(
        [
            own(input_weight[:, :full], 1, inner, spare * HEAD_DIM),
            input_weight[:, full : full + 2 * STATE],
            own(input_weight[:, full + 2 * STATE :], 1, hp, spare),
            jnp.zeros((input_weight.shape[0], width - inner - 2 * STATE - hp), BF16),
        ],
        axis=1,
    )
    cot = jnp.pad(output_grad[0], ((0, 0), (0, spare * HEAD_DIM))).T.reshape(seqs, inner, length)
    par = jnp.stack([own(v, 0, hp, spare) for v in (step_bias, decay_log, skip_gain)])
    par = jnp.broadcast_to(jnp.pad(par, ((0, 0), (0, slots - hp)))[:, :, None], (3, slots, 128))

    tokens, dy, columns, beside = collect(hidden[0], cot, weight, seqs, zeros)
    tokens = tokens.reshape(seqs * length, model)
    columns = columns.reshape(model, width)
    beside = beside.reshape(model, width)
    pre = lax.dot_general(columns, tokens, (((0,), (1,)), ((), ())), preferred_element_type=F32)
    grads, split, sums = mixer(pre, dy, par, hp)
    other = swap(split)

    def back(part, w):
        return lax.dot_general(part, w, (((1,), (1,)), ((), ())), preferred_element_type=F32)

    token_part = (back(split[0], columns) + back(other, beside)).astype(BF16)
    weight_part = lax.dot_general(
        tokens, grads, (((0,), (1,)), ((), ())), preferred_element_type=F32
    ).astype(BF16)
    every = seqs * zeros
    weight_part = weight_part.reshape(seqs, zeros, model // every, width)

    token_all, rows, sums_all = deliver(token_part, weight_part, sums, seqs, zeros)
    token_grad = jnp.sum(token_all.astype(F32), axis=0).astype(BF16)
    rows = rows.astype(F32)
    parts = rows.transpose(1, 0, 2)
    weight_grad = jnp.concatenate(
        [
            parts[:, :, :inner].reshape(-1, seqs * inner)[:, :full],
            jnp.sum(rows[:, :, inner : inner + 2 * STATE], axis=0),
            parts[:, :, inner + 2 * STATE : inner + 2 * STATE + hp].reshape(-1, seqs * hp)[:, :heads],
        ],
        axis=1,
    )
    sums_all = jnp.sum(sums_all.reshape(seqs, zeros, 3, slots, 128)[:, :, :, :hp, 0], axis=1)
    head_grads = sums_all.transpose(1, 0, 2).reshape(3, seqs * hp)[:, :heads]
    return (token_grad[None], weight_grad, head_grads)


def solution(mesh):
    placed = (P("zero", "seq", None), P("zero", "seq", None), P("zero", None), P(), P(), P())
    return jax.shard_map(
        functools.partial(body, mesh.shape["seq"], mesh.shape["zero"]),
        mesh=mesh,
        in_specs=placed,
        out_specs=(P("zero", "seq", None), P(("seq", "zero"), None), P()),
        check_vma=False,
    )
```

time: 141 us -> 135 us (0.957)
  Pallas kernels: 114 us -> 110 us
    pallas_call x1, Pallas kernels: 59.8 us -> 51.7 us  [deliver(): pl.pallas_call(functools.partial(deliver_kernel, seqs, zeros), out_shape=...]
    pallas_call x0 -> x1, Pallas kernels: none -> 4.38 us  [swap(): pl.pallas_call(swap_kernel, out_shape=jax.ShapeDtypeStruct(split.shape[1:...]
    pallas_call x1, Pallas kernels: 40.7 us -> 36.8 us  [collect(): pl.pallas_call(functools.partial(collect_kernel, seqs, zeros), out_shape=...]
    pallas_call x1, Pallas kernels: 13.9 us -> 17.1 us  [mixer(): pl.pallas_call(functools.partial(mixer_kernel, hp), out_shape=(jax.ShapeD...]
    dot_general x1 -> x2, matrix products: 3.77 us -> 3.54 us  [back(): lax.dot_general(part, w, (((1,), (1,)), ((), ())), preferred_element_type...]
where the time goes in v2:
time: 135 us
  Pallas kernels  110 us (81%)
  matrix products  11.2 us (8%)
  local copies, waits for them, and re-layouts  7.99 us (6%)
  other arithmetic  4.5 us (3%)
    pallas_call x1, Pallas kernels, deliver(): pl.pallas_call(functools.partial(deliver_kernel, seqs, zeros), out_shape=...  51.7 us
    pallas_call x1, Pallas kernels, collect(): pl.pallas_call(functools.partial(collect_kernel, seqs, zeros), out_shape=...  36.8 us
    pallas_call x1, Pallas kernels, mixer(): pl.pallas_call(functools.partial(mixer_kernel, hp), out_shape=(jax.ShapeD...  17.1 us
    pallas_call x1, Pallas kernels, swap(): pl.pallas_call(swap_kernel, out_shape=jax.ShapeDtypeStruct(split.shape[1:...  4.38 us
    dot_general x1, matrix products, body(): lax.dot_general(columns, tokens, (((0,), (1,)), ((), ())), preferred_elem...  4.2 us
    dot_general x2, matrix products, back(): lax.dot_general(part, w, (((1,), (1,)), ((), ())), preferred_element_type...  3.54 us
    dot_general x1, matrix products, body(): lax.dot_general(tokens, grads, (((0,), (1,)), ((), ())), preferred_elemen...  3.45 us

profile of v2, /device:TPU:9, one launch (start us, length us, event | category | flops | bytes accessed | tf_op | source)
XLA Modules:
  0.0 134.6 jit_solution(14484202998073613513)
XLA Ops:
  0.6 0.0 copy-start
  0.7 0.6 copy-done
  1.3 0.1 dynamic-slice_bitcast_fusion.2
  1.4 0.7 dynamic-slice_bitcast_fusion
  2.1 0.1 pad.14.clone
  2.2 0.1 broadcast_in_dim.13.par_ref
  2.3 0.9 slice.26
  3.2 0.1 constant_dynamic-slice_fusion
  3.3 2.2 %copy.18 = bf16[2560,128]{1,0:T(8,128)(2,1)} copy(bf16[2560,128]{0,1:T(8,128)(2,1)} %bitcast.39) | data formatting | bytes 1310720 | tf_op jit(solution)/shard_map/transpose | solution.py:493
  5.4 1.4 %slice-done.1 = bf16[320,2560]{1,0:T(8,128)(2,1)S(1)} async-done(((bf16[320,2856]{1,0:T(8,128)(2,1)}), bf16[320,2560]{1,0:T(8,128)(2,1)S(1)}, s32[]{:S(2)}) %slice-start.1) | async-done | bytes 1638424 | tf_op jit(solution)/shard_map/slice | solution.py:486
  6.9 0.1 constant_dynamic-slice_fusion.1
  7.0 0.0 slice-done
  7.0 0.9 maximum_maximum_fusion.wgt
  8.0 36.8 %collect.1 = (bf16[8,128,1280]{2,1,0:T(8,128)(2,1)}, bf16[8,320,128]{2,1,0:T(8,128)(2,1)}, bf16[4,320,640]{2,1,0:T(8,128)(2,1)}, bf16[4,320,640]{2,1,0:T(8,128)(2,1)}) custom-call(bf16[128,1280]{1,0:T(8,128)(2,1)} %bitcast.41, bf16[8,320,128]{2,1,0:T(8,128)(2,1)} %bitcast.36, bf16[320,640]{1,0:T(8,128)(2,1)} %maximum_maximum_fusion.wgt), custom_call_target="tpu_custom_call" | custom-call | tf_op jit(solution)/shard_map/collect/pallas_call | solution.py:163
  44.8 0.0 copy-start.3
  44.8 4.2 %fusion.5.pre_ref = f32[640,1024]{1,0:T(8,128)S(1)} fusion(bf16[1280,640]{1,0:T(8,128)(2,1)} %bitcast.46, bf16[1024,1280]{1,0:T(8,128)(2,1)} %bitcast.44), kind=kOutput, calls=%fused_computation.20 | convolution fusion | flops 1677721600 | bytes 6881280 | tf_op jit(solution)/shard_map/dot_general | solution.py:501
  49.0 0.0 copy-done.3
  49.0 0.0 copy-start.9
  49.0 17.1 %mixer.1 = (bf16[640,1024]{1,0:T(8,128)(2,1)S(1)}, bf16[2,4,640,128]{3,2,1,0:T(8,128)(2,1)S(1)}, f32[3,8,128]{2,1,0:T(8,128)S(1)}) custom-call(f32[640,1024]{1,0:T(8,128)S(1)} %fusion.5.pre_ref, bf16[8,320,128]{2,1,0:T(8,128)(2,1)S(1)} %copy-done.3, f32[3,8,128]{2,1,0:T(8,128)S(1)} %broadcast_in_dim.13.par_ref), custom_call_target="tpu_custom_call" | custom-call | tf_op jit(solution)/shard_map/mixer/pallas_call | solution.py:448
  66.1 0.0 copy-done.9
  66.2 3.4 %convolution_convert_fusion = bf16[1280,640]{1,0:T(8,128)(2,1)} fusion(bf16[1024,1280]{1,0:T(8,128)(2,1)S(1)} %bitcast.45, bf16[640,1024]{1,0:T(8,128)(2,1)S(1)} %get-tuple-element.18), kind=kOutput, calls=%fused_computation.1 | convolution fusion | flops 1678540800 | bytes 5570560 | tf_op jit(solution)/shard_map/dot_general | solution.py:509
  69.6 0.0 copy-done.1
  69.6 0.0 copy-done.4
  69.6 4.4 %swap.1 = bf16[4,640,128]{2,1,0:T(8,128)(2,1)} custom-call(bf16[2,4,640,128]{3,2,1,0:T(8,128)(2,1)} %copy-done.1), custom_call_target="tpu_custom_call" | custom-call | tf_op jit(solution)/shard_map/swap/pallas_call | solution.py:196
  74.0 0.0 copy-done.10
  74.0 0.0 copy-done.2
  74.0 0.0 copy-start.5
  74.0 0.0 copy-start.6
  74.0 1.2 fusion.1
  75.3 0.0 copy-done.5
  75.3 0.4 copy-done.6
  75.7 2.3 %fusion.tok = bf16[4,128,1280]{2,1,0:T(8,128)(2,1)} fusion(f32[4,128,1280]{2,1,0:T(8,128)S(1)} %fusion.1, bf16[4,640,128]{2,1,0:T(8,128)(2,1)S(1)} %copy-done.5, bf16[1280,640,1]{1,0,2:T(8,128)(2,1)S(1)} %bitcast.37), kind=kOutput, calls=%fused_computation.2 | convolution fusion | flops 840171520 | bytes 6225920 | tf_op jit(solution)/shard_map/dot_general | solution.py:506
  78.0 51.7 %deliver.1 = (bf16[4,128,1280]{2,1,0:T(8,128)(2,1)}, bf16[8,40,640]{2,1,0:T(8,128)(2,1)}, f32[32,3,8,128]{3,2,1,0:T(8,128)}) custom-call(bf16[4,128,1280]{2,1,0:T(8,128)(2,1)} %fusion.tok, bf16[8,4,40,640]{3,2,1,0:T(8,128)(2,1)} %bitcast.38, f32[3,8,128]{2,1,0:T(8,128)} %copy-done.4), custom_call_target="tpu_custom_call" | custom-call | tf_op jit(solution)/shard_map/deliver/pallas_call | solution.py:290
  129.7 0.0 copy-start.8
  129.7 0.0 copy-start.7
  129.7 2.4 %reduce_sum.30 = bf16[128,1280]{1,0:T(8,128)(2,1)} reduce(bf16[4,128,1280]{2,1,0:T(8,128)(2,1)} %get-tuple-element.20, bf16[]{:T(256)} %constant.20.clone.1), dimensions={0}, to_apply=%region_0.1 | reduce | flops 491520 | bytes 1638402 | tf_op jit(solution)/shard_map/reduce_sum | solution.py:516
  132.1 0.0 copy-done.8
  132.1 0.1 slice_reduce_fusion
  132.2 0.7 reshape.42
  132.9 0.0 copy-done.7
  132.9 0.1 fusion.4
  133.0 0.1 slice_reduce_fusion.1
  133.2 0.1 slice.34
  133.3 0.1 copy.22
  133.4 0.1 copy.23
  133.5 0.1 copy.21
  133.6 0.1 reshape.39
  133.8 0.8 pad_maximum_fusion
  (11 shorter events, 0.1 us)
Async XLA Ops:
  0.6 0.7 copy-start
  5.4 1.4 %slice-start.1 = ((bf16[320,2856]{1,0:T(8,128)(2,1)}), bf16[320,2560]{1,0:T(8,128)(2,1)S(1)}, s32[]{:S(2)}) async-start(bf16[320,2856]{1,0:T(8,128)(2,1)} %param.8), calls=%async_computation.1 | async-start | bytes 3276800 | tf_op jit(solution)/shard_map/slice | solution.py:486
  5.4 1.6 %slice-start = ((bf16[320,2856]{1,0:T(8,128)(2,1)}), bf16[320,256]{1,0:T(8,128)(2,1)S(1)}, s32[]{:S(2)}) async-start(bf16[320,2856]{1,0:T(8,128)(2,1)} %param.8), calls=%async_computation | async-start | bytes 327680 | tf_op jit(solution)/shard_map/slice | solution.py:487
  44.8 4.2 %copy-start.3 = (bf16[8,320,128]{2,1,0:T(8,128)(2,1)S(1)}, bf16[8,320,128]{2,1,0:T(8,128)(2,1)}, u32[]{:S(2)}) copy-start(bf16[8,320,128]{2,1,0:T(8,128)(2,1)} %get-tuple-element.15.dy_ref) | copy-start | bytes 1966084
  49.0 17.1 %copy-start.9 = (bf16[8,128,1280]{2,1,0:T(8,128)(2,1)S(1)}, bf16[8,128,1280]{2,1,0:T(8,128)(2,1)}, u32[]{:S(2)}) copy-start(bf16[8,128,1280]{2,1,0:T(8,128)(2,1)} %get-tuple-element.14) | copy-start | bytes 7864324
  66.1 3.5 %copy-start.1 = (bf16[2,4,640,128]{3,2,1,0:T(8,128)(2,1)}, bf16[2,4,640,128]{3,2,1,0:T(8,128)(2,1)S(1)}, u32[]{:S(2)}) copy-start(bf16[2,4,640,128]{3,2,1,0:T(8,128)(2,1)S(1)} %get-tuple-element.16.give) | copy-start | bytes 3932164
  66.1 3.5 %copy-start.4 = (f32[3,8,128]{2,1,0:T(8,128)}, f32[3,8,128]{2,1,0:T(8,128)S(1)}, u32[]{:S(2)}) copy-start(f32[3,8,128]{2,1,0:T(8,128)S(1)} %get-tuple-element.19.head) | copy-start | bytes 36868
  66.1 7.9 %copy-start.10 = (bf16[4,320,640]{2,1,0:T(8,128)(2,1)S(1)}, bf16[4,320,640]{2,1,0:T(8,128)(2,1)}, u32[]{:S(2)}) copy-start(bf16[4,320,640]{2,1,0:T(8,128)(2,1)} %get-tuple-element.13) | copy-start | bytes 4915204
  69.6 4.4 %copy-start.2 = (bf16[2,4,640,128]{3,2,1,0:T(8,128)(2,1)S(1)}, bf16[2,4,640,128]{3,2,1,0:T(8,128)(2,1)}, u32[]{:S(2)}) copy-start(bf16[2,4,640,128]{3,2,1,0:T(8,128)(2,1)} %copy-done.1) | copy-start | bytes 3932164
  74.0 1.3 copy-start.5
  74.0 1.6 %copy-start.6 = (bf16[4,320,640]{2,1,0:T(8,128)(2,1)S(1)}, bf16[4,320,640]{2,1,0:T(8,128)(2,1)}, u32[]{:S(2)}) copy-start(bf16[4,320,640]{2,1,0:T(8,128)(2,1)} %get-tuple-element.17) | copy-start | bytes 4915204
  129.7 2.4 %copy-start.8 = (f32[32,3,8,128]{3,2,1,0:T(8,128)S(1)}, f32[32,3,8,128]{3,2,1,0:T(8,128)}, u32[]{:S(2)}) copy-start(f32[32,3,8,128]{3,2,1,0:T(8,128)} %get-tuple-element.22) | copy-start | bytes 1179652
  129.7 3.2 %copy-start.7 = (bf16[8,40,640]{2,1,0:T(8,128)(2,1)S(1)}, bf16[8,40,640]{2,1,0:T(8,128)(2,1)}, u32[]{:S(2)}) copy-start(bf16[8,40,640]{2,1,0:T(8,128)(2,1)} %get-tuple-element.21) | copy-start | bytes 1228804

commit v3 on v2

--- a/solution.py
+++ b/solution.py
@@ -183,25 +183,35 @@
     )(tok, cot, wgt)
 
 
-def swap_kernel(give, got, send, recv):
+def swap_kernel(give, maps, got, got_map, send, recv):
     me_s, me_z = lax.axis_index("seq"), lax.axis_index("zero")
-    sibling = (me_s // 2 * 2 + 1 - lax.rem(me_s, 2), me_z)
+    core = lax.rem(me_s, 2)
+    sibling = (me_s // 2 * 2 + 1 - core, me_z)
     greet([sibling])
-    copy = remote(give.at[1], got, send, recv, sibling)
-    copy.start()
-    copy.wait()
-
-
-def swap(split):
+    copies = [
+        remote(maps.at[1 - core], got_map, send.at[0], recv.at[0], sibling),
+        remote(give.at[1], got, send.at[1], recv.at[1], sibling),
+    ]
+    for copy in copies:
+        copy.start()
+    for copy in copies:
+        copy.wait()
+
+
+def swap(split, maps):
+    vmem = pl.BlockSpec(memory_space=pltpu.VMEM)
     return pl.pallas_call(
         swap_kernel,
-        out_shape=jax.ShapeDtypeStruct(split.shape[1:], split.dtype),
-        in_specs=[pl.BlockSpec(memory_space=pltpu.VMEM)],
-        out_specs=pl.BlockSpec(memory_space=pltpu.VMEM),
-        scratch_shapes=[pltpu.SemaphoreType.DMA, pltpu.SemaphoreType.DMA],
+        out_shape=(
+            jax.ShapeDtypeStruct(split.shape[1:], split.dtype),
+            jax.ShapeDtypeStruct(maps.shape[1:], maps.dtype),
+        ),
+        in_specs=[vmem, vmem],
+        out_specs=(vmem, vmem),
+        scratch_shapes=[pltpu.SemaphoreType.DMA((2,)), pltpu.SemaphoreType.DMA((2,))],
         compiler_params=pltpu.CompilerParams(collective_id=2, has_side_effects=True),
         name="swap",
-    )(split)
+    )(split, maps)
 
 
 def deliver_kernel(
@@ -310,7 +320,7 @@
     )(tok, wgt, head)
 
 
-def mixer_kernel(hp, pre_ref, dy_ref, par_ref, g_ref, split_ref, head_ref, states, grad, acc):
+def mixer_kernel(hp, pre_ref, dy_ref, par_ref, g_ref, split_ref, maps_ref, head_ref, states, grad, acc):
     chunks, inner, group = dy_ref.shape
     top = inner + 2 * STATE
     slots = acc.shape[1]
@@ -419,7 +429,7 @@
 
         slope = sig * (1.0 + pre * (1.0 - sig))
         map_slope = map_sig * (1.0 + maps * (1.0 - map_sig))
-        rest = g_ref.shape[0] - top - slots
+        rest = g_ref.shape[0] - inner - STATE - slots
         rounded = jnp.concatenate(
             [
                 (du * spread(step) + dy * gain_full) * slope,
@@ -429,7 +439,11 @@
             ],
             axis=0,
         ).astype(BF16)
-        g_ref[:, at] = rounded
+        maps_ref[0, :, at] = d_in * map_slope[:STATE]
+        maps_ref[1, :, at] = d_out * map_slope[STATE:]
+        g_ref[:inner, at] = rounded[:inner]
+        g_ref[inner : inner + STATE, at] = jnp.zeros((STATE, group), BF16)
+        g_ref[inner + STATE :, at] = rounded[top:]
         split_ref[lax.rem(k + core, 2), k // 2] = rounded
         acc[0] += d_raw
         acc[1] += d_log * (rate * step)
@@ -448,12 +462,13 @@
     return pl.pallas_call(
         functools.partial(mixer_kernel, hp),
         out_shape=(
-            jax.ShapeDtypeStruct(pre.shape, BF16),
+            jax.ShapeDtypeStruct((pre.shape[0] - STATE, pre.shape[1]), BF16),
             jax.ShapeDtypeStruct((2, chunks // 2, pre.shape[0], group), BF16),
+            jax.ShapeDtypeStruct((2, STATE, pre.shape[1]), F32),
             jax.ShapeDtypeStruct((3, slots, 128), F32),
         ),
         in_specs=[pl.BlockSpec(memory_space=pltpu.VMEM)] * 3,
-        out_specs=(pl.BlockSpec(memory_space=pltpu.VMEM),) * 3,
+        out_specs=(pl.BlockSpec(memory_space=pltpu.VMEM),) * 4,
         scratch_shapes=[
             pltpu.VMEM((chunks, inner, STATE), F32),
             pltpu.VMEM((inner, STATE), F32),
@@ -470,8 +485,10 @@
     slots = up(hp, 8)
     inner, full = hp * HEAD_DIM, heads * HEAD_DIM
     spare = seqs * hp - heads
-    width = up(inner + 2 * STATE + slots, 128)
+    width = up(inner + STATE + slots, 128)
     me = lax.axis_index("seq")
+    core = lax.rem(me, 2)
+    mine = inner + STATE
     length, model = hidden.shape[1:]
 
     def own(array, axis, size, extra):
@@ -484,9 +501,9 @@
     weight = jnp.concatenate(
         [
             own(input_weight[:, :full], 1, inner, spare * HEAD_DIM),
-            input_weight[:, full : full + 2 * STATE],
+            lax.dynamic_slice_in_dim(input_weight[:, full : full + 2 * STATE], core * STATE, STATE, 1),
             own(input_weight[:, full + 2 * STATE :], 1, hp, spare),
-            jnp.zeros((input_weight.shape[0], width - inner - 2 * STATE - hp), BF16),
+            jnp.zeros((input_weight.shape[0], width - mine - hp), BF16),
         ],
         axis=1,
     )
@@ -498,9 +515,15 @@
     tokens = tokens.reshape(seqs * length, model)
     columns = columns.reshape(model, width)
     beside = beside.reshape(model, width)
+    here, there = columns[:, inner:mine], beside[:, inner:mine]
+    both = [jnp.where(core == 0, here, there), jnp.where(core == 0, there, here)]
+    columns = jnp.concatenate([columns[:, :inner]] + both + [columns[:, mine:]], axis=1)
+    beside = jnp.concatenate([beside[:, :inner]] + both + [beside[:, mine:]], axis=1)
     pre = lax.dot_general(columns, tokens, (((0,), (1,)), ((), ())), preferred_element_type=F32)
-    grads, split, sums = mixer(pre, dy, par, hp)
-    other = swap(split)
+    grads, split, maps, sums = mixer(pre, dy, par, hp)
+    other, other_map = swap(split, maps)
+    pair_map = lax.dynamic_index_in_dim(maps, core, 0, False) + other_map
+    grads = jnp.concatenate([grads[:inner], pair_map.astype(BF16), grads[mine:]], axis=0)
 
     def back(part, w):
         return lax.dot_general(part, w, (((1,), (1,)), ((), ())), preferred_element_type=F32)
@@ -519,8 +542,9 @@
     weight_grad = jnp.concatenate(
         [
             parts[:, :, :inner].reshape(-1, seqs * inner)[:, :full],
-            jnp.sum(rows[:, :, inner : inner + 2 * STATE], axis=0),
-            parts[:, :, inner + 2 * STATE : inner + 2 * STATE + hp].reshape(-1, seqs * hp)[:, :heads],
+            jnp.sum(rows[0::2, :, inner:mine], axis=0),
+            jnp.sum(rows[1::2, :, inner:mine], axis=0),
+            parts[:, :, mine : mine + hp].reshape(-1, seqs * hp)[:, :heads],
         ],
         axis=1,
     )

time: 135 us -> 133 us (0.985)
  Pallas kernels: 110 us -> 99.8 us
  local copies, waits for them, and re-layouts: 7.99 us -> 12.2 us
  other arithmetic: 4.5 us -> 6.83 us
  matrix products: 11.2 us -> 12.9 us
    pallas_call x1, Pallas kernels: 51.7 us -> 43.9 us  [deliver(): pl.pallas_call(functools.partial(deliver_kernel, seqs, zeros), out_shape=...]
    pallas_call x1, Pallas kernels: 36.8 us -> 31.2 us  [collect(): pl.pallas_call(functools.partial(collect_kernel, seqs, zeros), out_shape=...]
    unnamed x22 -> x46, local copies, waits for them, and re-layouts: 1.06 us -> 4.29 us
    slice x2 -> x8, local copies, waits for them, and re-layouts: 0.21 us -> 3.28 us  [the longest x1 1.4 us: body(): columns[:, :inner]]
    pallas_call x1, Pallas kernels: 17.1 us -> 19 us  [mixer(): pl.pallas_call(functools.partial(mixer_kernel, hp), out_shape=(jax.ShapeD...]
    dot_general x1, matrix products: 4.2 us -> 5.82 us  [body(): lax.dot_general(columns, tokens, (((0,), (1,)), ((), ())), preferred_elem...]
    select_n x0 -> x1, other arithmetic: none -> 1.53 us  [body(): jnp.where(core == 0, here, there)]
    slice x2, local copies, waits for them, and re-layouts: 1.43 us -> 0.01 us  [body(): input_weight[:, :full]]
where the time goes in v3:
time: 133 us
  Pallas kernels  99.8 us (75%)
  matrix products  12.9 us (10%)
  local copies, waits for them, and re-layouts  12.2 us (9%)
  other arithmetic  6.83 us (5%)
    pallas_call x1, Pallas kernels, deliver(): pl.pallas_call(functools.partial(deliver_kernel, seqs, zeros), out_shape=...  43.9 us
    pallas_call x1, Pallas kernels, collect(): pl.pallas_call(functools.partial(collect_kernel, seqs, zeros), out_shape=...  31.2 us
    pallas_call x1, Pallas kernels, mixer(): pl.pallas_call(functools.partial(mixer_kernel, hp), out_shape=(jax.ShapeD...  19 us
    dot_general x1, matrix products, body(): lax.dot_general(columns, tokens, (((0,), (1,)), ((), ())), preferred_elem...  5.82 us
    pallas_call x1, Pallas kernels, swap(): pl.pallas_call(swap_kernel, out_shape=(jax.ShapeDtypeStruct(split.shape[1...  5.65 us
    dot_general x2, matrix products, back(): lax.dot_general(part, w, (((1,), (1,)), ((), ())), preferred_element_type...  4.44 us
    unnamed x46, local copies, waits for them, and re-layouts  4.29 us
    dot_general x1, matrix products, body(): lax.dot_general(tokens, grads, (((0,), (1,)), ((), ())), preferred_elemen...  2.68 us

profile of v3, /device:TPU:9, one launch (start us, length us, event | category | flops | bytes accessed | tf_op | source)
XLA Modules:
  0.0 132.8 jit_solution(9285345807646264293)
XLA Ops:
  0.6 0.0 copy-start
  0.6 0.0 slice-start
  0.7 1.0 slice.52
  1.7 0.9 slice.53
  2.6 0.1 constant_dynamic-slice_fusion
  2.7 0.0 copy-start.11
  2.8 0.1 constant_dynamic-slice_fusion.2
  2.9 0.1 pad.26.clone
  3.0 0.9 maximum_maximum_fusion.wgt
  3.9 1.1 copy.18
  5.0 31.2 %collect.1 = (bf16[8,128,1280]{2,1,0:T(8,128)(2,1)}, bf16[8,320,128]{2,1,0:T(8,128)(2,1)}, bf16[4,320,512]{2,1,0:T(8,128)(2,1)}, bf16[4,320,512]{2,1,0:T(8,128)(2,1)}) custom-call(bf16[128,1280]{1,0:T(8,128)(2,1)} %bitcast.48, bf16[8,320,128]{2,1,0:T(8,128)(2,1)} %bitcast.38, bf16[320,512]{1,0:T(8,128)(2,1)} %maximum_maximum_fusion.wgt), custom_call_target="tpu_custom_call" | custom-call | tf_op jit(solution)/shard_map/collect/pallas_call | solution.py:163
  36.2 1.4 %slice.68 = bf16[1280,320]{1,0:T(8,128)(2,1)S(1)} slice(bf16[1280,512]{1,0:T(8,128)(2,1)} %bitcast.42), slice={[0:1280], [0:320]} | slice | bytes 1638400 | tf_op jit(solution)/shard_map/slice | solution.py:520
  37.6 0.2 copy-done.7
  37.8 1.5 %broadcast_select_fusion.1 = (bf16[1280,128]{1,0:T(8,128)(2,1)S(1)}, bf16[1280,128]{1,0:T(8,128)(2,1)S(1)}) fusion(pred[]{:T(512)S(6)} %eq.4, bf16[1280,512]{1,0:T(8,128)(2,1)S(1)} %bitcast.39, bf16[1280,512]{1,0:T(8,128)(2,1)} %bitcast.43), kind=kLoop, calls=%fused_computation.27 | loop fusion | flops 327680 | bytes 1310721 | tf_op jit(solution)/shard_map/jit(_where)/select_n | solution.py:519
  39.3 0.0 copy-start.15
  39.3 0.0 copy-start.17
  39.4 1.4 %slice.71 = bf16[1280,64]{1,0:T(8,128)(2,1)S(1)} slice(bf16[1280,512]{1,0:T(8,128)(2,1)} %bitcast.44), slice={[0:1280], [448:512]} | slice | bytes 327680 | tf_op jit(solution)/shard_map/slice | solution.py:520
  40.7 0.0 copy-start.19
  40.7 0.0 copy-start.20
  40.8 5.8 %fusion.18.pre_ref = f32[640,1024]{1,0:T(8,128)} fusion(bf16[1024,1280]{1,0:T(8,128)(2,1)} %bitcast.51, bf16[1280,128]{1,0:T(8,128)(2,1)S(1)} %get-tuple-element.32, bf16[1280,128]{1,0:T(8,128)(2,1)S(1)} %get-tuple-element.31, bf16[1280,64]{1,0:T(8,128)(2,1)S(1)} %slice.71, bf16[1280,320]{1,0:T(8,128)(2,1)S(1)} %slice.68), kind=kOutput, calls=%fused_computation.29 | convolution fusion | flops 1684275200 | bytes 6881280 | tf_op jit(solution)/shard_map/dot_general | solution.py:522
  46.6 0.1 dynamic-slice_bitcast_fusion
  46.7 0.1 dynamic-slice_bitcast_fusion.2
  46.8 0.1 broadcast_in_dim.13.par_ref
  46.9 19.0 %mixer.1 = (bf16[512,1024]{1,0:T(8,128)(2,1)S(1)}, bf16[2,4,640,128]{3,2,1,0:T(8,128)(2,1)S(1)}, f32[2,128,1024]{2,1,0:T(8,128)S(1)}, f32[3,8,128]{2,1,0:T(8,128)S(1)}) custom-call(f32[640,1024]{1,0:T(8,128)} %fusion.18.pre_ref, bf16[8,320,128]{2,1,0:T(8,128)(2,1)S(1)} %copy-done.5, f32[3,8,128]{2,1,0:T(8,128)S(1)} %broadcast_in_dim.13.par_ref), custom_call_target="tpu_custom_call" | custom-call | tf_op jit(solution)/shard_map/mixer/pallas_call | solution.py:462
  65.9 1.0 copy-done.1
  66.9 1.1 copy-done.3
  68.0 0.6 copy-done.6
  68.6 5.7 %swap.1 = (bf16[4,640,128]{2,1,0:T(8,128)(2,1)}, f32[128,1024]{1,0:T(8,128)}) custom-call(bf16[2,4,640,128]{3,2,1,0:T(8,128)(2,1)} %copy-done.3, f32[2,128,1024]{2,1,0:T(8,128)} %copy-done.1), custom_call_target="tpu_custom_call" | custom-call | tf_op jit(solution)/shard_map/swap/pallas_call | solution.py:203
  74.2 1.3 fusion.16
  75.6 0.5 copy-done.21
  76.2 2.7 %convolution_convert_fusion = bf16[1280,512]{1,0:T(8,128)(2,1)} fusion(bf16[1024,1280]{1,0:T(8,128)(2,1)S(1)} %bitcast.52, bf16[64,1024]{1,0:T(8,128)(2,1)S(1)} %slice.62, bf16[128,1024]{1,0:T(8,128)(2,1)S(1)} %fusion.16, bf16[320,1024]{1,0:T(8,128)(2,1)S(1)} %slice.61), kind=kOutput, calls=%fused_computation.2 | convolution fusion | flops 1345978368 | bytes 4980736 | tf_op jit(solution)/shard_map/dot_general | solution.py:532
  78.9 1.7 %fusion.7 = f32[4,128,1280]{2,1,0:T(8,128)S(1)} fusion(bf16[2,4,640,128]{3,2,1,0:T(8,128)(2,1)S(1)} %copy-done.4, bf16[1280,128]{1,0:T(8,128)(2,1)S(1)} %copy-done.18, bf16[1280,128]{1,0:T(8,128)(2,1)S(1)} %copy-done.16, bf16[1280,64]{1,0:T(8,128)(2,1)S(1)} %copy-done.14, bf16[1280,320]{1,0:T(8,128)(2,1)S(1)} %copy-done.10), kind=kOutput, calls=%fused_computation.12 | convolution fusion | flops 845414400 | bytes 5242880 | tf_op jit(solution)/shard_map/dot_general | solution.py:529
  80.5 0.1 slice.72
  80.7 0.2 slice.73
  80.8 0.8 copy-done.22
  81.6 2.8 %fusion.tok = bf16[4,128,1280]{2,1,0:T(8,128)(2,1)} fusion(f32[4,128,1280]{2,1,0:T(8,128)S(1)} %fusion.7, bf16[4,640,128]{2,1,0:T(8,128)(2,1)S(1)} %copy-done.22, bf16[1280,128]{1,0:T(8,128)(2,1)S(1)} %copy-done.18, bf16[1280,128]{1,0:T(8,128)(2,1)S(1)} %copy-done.16, bf16[1280,64]{1,0:T(8,128)(2,1)S(1)} %slice.73, bf16[1280,320]{1,0:T(8,128)(2,1)S(1)} %slice.72), kind=kOutput, calls=%fused_computation.1 | convolution fusion | flops 846725120 | bytes 6225920 | tf_op jit(solution)/shard_map/dot_general | solution.py:529
  84.4 43.9 %deliver.1 = (bf16[4,128,1280]{2,1,0:T(8,128)(2,1)}, bf16[8,40,512]{2,1,0:T(8,128)(2,1)}, f32[32,3,8,128]{3,2,1,0:T(8,128)}) custom-call(bf16[4,128,1280]{2,1,0:T(8,128)(2,1)} %fusion.tok, bf16[8,4,40,512]{3,2,1,0:T(8,128)(2,1)} %bitcast.45, f32[3,8,128]{2,1,0:T(8,128)} %copy-done.6), custom_call_target="tpu_custom_call" | custom-call | tf_op jit(solution)/shard_map/deliver/pallas_call | solution.py:300
  128.3 1.1 fusion.24
  129.5 0.1 copy.21
  129.6 0.1 reshape.39
  129.7 0.1 slice.75
  129.9 0.1 copy.22
  130.0 0.1 copy.23
  130.1 0.1 slice_reduce_fusion.2
  130.2 0.8 pad_maximum_fusion.4
  131.0 1.0 reduce_sum.39
  132.0 0.1 slice_reduce_fusion
  132.1 0.7 reshape.42
  (43 shorter events, 0.2 us)
Async XLA Ops:
  0.6 46.1 %copy-start = (f32[40]{0:T(128)S(1)}, f32[40]{0:T(128)}, u32[]{:S(2)}) copy-start(f32[40]{0:T(128)} %param.9) | copy-start | bytes 484
  0.6 2.1 %slice-start = ((bf16[320,2856]{1,0:T(8,128)(2,1)}), bf16[320,2560]{1,0:T(8,128)(2,1)S(1)}, s32[]{:S(2)}) async-start(bf16[320,2856]{1,0:T(8,128)(2,1)} %param.8), calls=%async_computation | async-start | bytes 3276800 | tf_op jit(solution)/shard_map/slice | solution.py:503
  2.7 1.1 copy-start.11
  36.2 1.6 %copy-start.7 = (bf16[4,320,512]{2,1,0:T(8,128)(2,1)S(1)}, bf16[4,320,512]{2,1,0:T(8,128)(2,1)}, u32[]{:S(2)}) copy-start(bf16[4,320,512]{2,1,0:T(8,128)(2,1)} %get-tuple-element.17) | copy-start | bytes 3932164
  37.6 9.0 %copy-start.9 = (bf16[1280,320]{1,0:T(8,128)(2,1)}, bf16[1280,320]{1,0:T(8,128)(2,1)S(1)}, u32[]{:S(2)}) copy-start(bf16[1280,320]{1,0:T(8,128)(2,1)S(1)} %slice.68) | copy-start | bytes 2457604
  39.3 7.3 %copy-start.15 = (bf16[1280,128]{1,0:T(8,128)(2,1)}, bf16[1280,128]{1,0:T(8,128)(2,1)S(1)}, u32[]{:S(2)}) copy-start(bf16[1280,128]{1,0:T(8,128)(2,1)S(1)} %get-tuple-element.31) | copy-start | bytes 983044
  39.3 7.2 %copy-start.17 = (bf16[1280,128]{1,0:T(8,128)(2,1)}, bf16[1280,128]{1,0:T(8,128)(2,1)S(1)}, u32[]{:S(2)}) copy-start(bf16[1280,128]{1,0:T(8,128)(2,1)S(1)} %get-tuple-element.32) | copy-start | bytes 983044
  40.7 5.9 %copy-start.13 = (bf16[1280,64]{1,0:T(8,128)(2,1)}, bf16[1280,64]{1,0:T(8,128)(2,1)S(1)}, u32[]{:S(2)}) copy-start(bf16[1280,64]{1,0:T(8,128)(2,1)S(1)} %slice.71) | copy-start | bytes 491524
  40.7 5.9 %copy-start.19 = (f32[40]{0:T(128)S(1)}, f32[40]{0:T(128)}, u32[]{:S(2)}) copy-start(f32[40]{0:T(128)} %param.11) | copy-start | bytes 484
  40.7 5.9 %copy-start.20 = (f32[40]{0:T(128)S(1)}, f32[40]{0:T(128)}, u32[]{:S(2)}) copy-start(f32[40]{0:T(128)} %param.10) | copy-start | bytes 484
  40.8 6.1 %copy-start.5 = (bf16[8,320,128]{2,1,0:T(8,128)(2,1)S(1)}, bf16[8,320,128]{2,1,0:T(8,128)(2,1)}, u32[]{:S(2)}) copy-start(bf16[8,320,128]{2,1,0:T(8,128)(2,1)} %get-tuple-element.19.dy_ref) | copy-start | bytes 1966084
  65.9 1.0 copy-start.1
  66.9 1.1 copy-start.3
  68.0 0.6 copy-start.6
  68.6 5.7 %copy-start.2 = (f32[2,128,1024]{2,1,0:T(8,128)S(1)}, f32[2,128,1024]{2,1,0:T(8,128)}, u32[]{:S(2)}) copy-start(f32[2,128,1024]{2,1,0:T(8,128)} %copy-done.1) | copy-start | bytes 3145732
  74.2 1.9 %copy-start.21 = (bf16[8,128,1280]{2,1,0:T(8,128)(2,1)S(1)}, bf16[8,128,1280]{2,1,0:T(8,128)(2,1)}, u32[]{:S(2)}) copy-start(bf16[8,128,1280]{2,1,0:T(8,128)(2,1)} %get-tuple-element.18) | copy-start | bytes 7864324
  76.1 2.7 %copy-start.4 = (bf16[2,4,640,128]{3,2,1,0:T(8,128)(2,1)S(1)}, bf16[2,4,640,128]{3,2,1,0:T(8,128)(2,1)}, u32[]{:S(2)}) copy-start(bf16[2,4,640,128]{3,2,1,0:T(8,128)(2,1)} %copy-done.3) | copy-start | bytes 3932164
  76.1 2.7 %copy-start.10 = (bf16[1280,320]{1,0:T(8,128)(2,1)S(1)}, bf16[1280,320]{1,0:T(8,128)(2,1)}, u32[]{:S(2)}) copy-start(bf16[1280,320]{1,0:T(8,128)(2,1)} %copy-done.9) | copy-start | bytes 2457604
  76.1 2.7 %copy-start.14 = (bf16[1280,64]{1,0:T(8,128)(2,1)S(1)}, bf16[1280,64]{1,0:T(8,128)(2,1)}, u32[]{:S(2)}) copy-start(bf16[1280,64]{1,0:T(8,128)(2,1)} %copy-done.13) | copy-start | bytes 491524
  76.1 2.7 %copy-start.16 = (bf16[1280,128]{1,0:T(8,128)(2,1)S(1)}, bf16[1280,128]{1,0:T(8,128)(2,1)}, u32[]{:S(2)}) copy-start(bf16[1280,128]{1,0:T(8,128)(2,1)} %copy-done.15) | copy-start | bytes 983044
  76.1 2.7 %copy-start.18 = (bf16[1280,128]{1,0:T(8,128)(2,1)S(1)}, bf16[1280,128]{1,0:T(8,128)(2,1)}, u32[]{:S(2)}) copy-start(bf16[1280,128]{1,0:T(8,128)(2,1)} %copy-done.17) | copy-start | bytes 983044
  80.5 1.1 copy-start.22
  129.4 1.6 %copy-start.8 = (bf16[4,128,1280]{2,1,0:T(8,128)(2,1)S(1)}, bf16[4,128,1280]{2,1,0:T(8,128)(2,1)}, u32[]{:S(2)}) copy-start(bf16[4,128,1280]{2,1,0:T(8,128)(2,1)} %get-tuple-element.26) | copy-start | bytes 3932164
  129.9 2.1 %copy-start.12 = (f32[32,3,8,128]{3,2,1,0:T(8,128)S(1)}, f32[32,3,8,128]{3,2,1,0:T(8,128)}, u32[]{:S(2)}) copy-start(f32[32,3,8,128]{3,2,1,0:T(8,128)} %get-tuple-element.28) | copy-start | bytes 1179652

commit v4 on v3

--- a/solution.py
+++ b/solution.py
@@ -199,15 +199,15 @@
 
 
 def swap(split, maps):
-    vmem = pl.BlockSpec(memory_space=pltpu.VMEM)
+    anywhere = pl.BlockSpec(memory_space=pl.ANY)
     return pl.pallas_call(
         swap_kernel,
         out_shape=(
             jax.ShapeDtypeStruct(split.shape[1:], split.dtype),
             jax.ShapeDtypeStruct(maps.shape[1:], maps.dtype),
         ),
-        in_specs=[vmem, vmem],
-        out_specs=(vmem, vmem),
+        in_specs=[anywhere, anywhere],
+        out_specs=(anywhere, anywhere),
         scratch_shapes=[pltpu.SemaphoreType.DMA((2,)), pltpu.SemaphoreType.DMA((2,))],
         compiler_params=pltpu.CompilerParams(collective_id=2, has_side_effects=True),
         name="swap",
@@ -216,36 +216,22 @@
 
 def deliver_kernel(
     seqs, zeros, tok, wgt, head, tok_out, wgt_out, head_out,
-    zin, zsum, tsem, zsem, wsem, hsem, loc,
+    zin, zsum, hin, hsum, tsem, zsem, wsem, hsem, gsem, loc,
 ):
     me_s, me_z = lax.axis_index("seq"), lax.axis_index("zero")
-    every = seqs * zeros
-    me = me_s * zeros + me_z
     chips = seqs // 2
     chip, core = me_s // 2, lax.rem(me_s, 2)
-
-    def anyone(step):
-        target = lax.rem(me + step, every)
-        return (target // zeros, lax.rem(target, zeros))
-
-    barrier = pltpu.get_barrier_semaphore()
-
-    def signal(step, carry):
-        pl.semaphore_signal(barrier, inc=1, device_id=anyone(step), device_id_type=MESH)
-        return carry
-
-    lax.fori_loop(1, every, signal, 0)
-    pl.semaphore_wait(barrier, every - 1)
-
-    def head_copy(step):
-        return remote(head, head_out.at[me], hsem.at[0, step], hsem.at[1, step], anyone(step))
-
+    greet(
+        [(me_s, lax.rem(me_z + d, zeros)) for d in range(1, zeros)]
+        + [(lax.rem(me_s + d, seqs), me_z) for d in range(1, seqs)]
+    )
     across = []
     for d in range(1, zeros):
         target = lax.rem(me_z + d, zeros)
         across.append(
             remote(wgt.at[:, target], zin.at[d], zsem.at[0, d], zsem.at[1, d], (me_s, target))
         )
+        across.append(remote(head, hin.at[d], hsem.at[0, d], hsem.at[1, d], (me_s, target)))
     tokens = []
     for d in range(1, chips):
         target = lax.rem(chip + d, chips)
@@ -255,18 +241,19 @@
                 (target * 2 + core, me_z),
             )
         )
-    own = [
-        pltpu.make_async_copy(tok.at[chip], tok_out.at[chip], loc.at[0]),
-        pltpu.make_async_copy(head, head_out.at[me], loc.at[1]),
+    own = [pltpu.make_async_copy(tok.at[chip], tok_out.at[chip], loc.at[0])]
+    first = [
+        pltpu.make_async_copy(wgt.at[:, me_z], zin.at[0], loc.at[2]),
+        pltpu.make_async_copy(head, hin.at[0], loc.at[1]),
     ]
-    first = pltpu.make_async_copy(wgt.at[:, me_z], zin.at[0], loc.at[2])
-    first.start()
-    for copy in across + tokens + own:
-        copy.start()
-    lax.fori_loop(1, every, lambda i, c: (head_copy(i).start(), c)[1], 0)
-    first.wait()
-    for copy in across:
+    for copy in across + tokens + first + own:
+        copy.start()
+    for copy in first + across:
         copy.wait()
+    sums = hin[0]
+    for d in range(1, zeros):
+        sums = sums + hin[d]
+    hsum[...] = sums
 
     def add(j, carry):
         total = zin[0, j].astype(F32)
@@ -276,8 +263,12 @@
         return carry
 
     lax.fori_loop(0, seqs, add, 0)
-    last = pltpu.make_async_copy(zsum.at[me_s], wgt_out.at[me_s], loc.at[3])
-    last.start()
+    own += [
+        pltpu.make_async_copy(zsum.at[me_s], wgt_out.at[me_s], loc.at[3]),
+        pltpu.make_async_copy(hsum, head_out.at[me_s], loc.at[4]),
+    ]
+    for copy in own[1:]:
+        copy.start()
     along = []
     for d in range(1, seqs):
         target = lax.rem(me_s + d, seqs)
@@ -286,34 +277,38 @@
                 zsum.at[target], wgt_out.at[me_s], wsem.at[0, d], wsem.at[1, d], (target, me_z)
             )
         )
+        along.append(
+            remote(hsum, head_out.at[me_s], gsem.at[0, d], gsem.at[1, d], (target, me_z))
+        )
     for copy in along:
         copy.start()
-    for copy in own + [last] + tokens + along:
+    for copy in own + tokens + along:
         copy.wait()
-    lax.fori_loop(1, every, lambda i, c: (head_copy(i).wait(), c)[1], 0)
 
 
 def deliver(tok, wgt, head, seqs, zeros):
     anywhere = pl.BlockSpec(memory_space=pl.ANY)
-    every = seqs * zeros
     block = wgt.shape[2:]
     return pl.pallas_call(
         functools.partial(deliver_kernel, seqs, zeros),
         out_shape=(
             jax.ShapeDtypeStruct(tok.shape, tok.dtype),
             jax.ShapeDtypeStruct((seqs,) + block, wgt.dtype),
-            jax.ShapeDtypeStruct((every,) + head.shape, head.dtype),
+            jax.ShapeDtypeStruct((seqs,) + head.shape, head.dtype),
         ),
         in_specs=[anywhere] * 3,
         out_specs=(anywhere,) * 3,
         scratch_shapes=[
             pltpu.VMEM((zeros, seqs) + block, BF16),
             pltpu.VMEM((seqs,) + block, BF16),
+            pltpu.VMEM((zeros,) + head.shape, F32),
+            pltpu.VMEM(head.shape, F32),
             pltpu.SemaphoreType.DMA((2, seqs)),
             pltpu.SemaphoreType.DMA((2, zeros)),
             pltpu.SemaphoreType.DMA((2, seqs)),
-            pltpu.SemaphoreType.DMA((2, every)),
-            pltpu.SemaphoreType.DMA((4,)),
+            pltpu.SemaphoreType.DMA((2, zeros)),
+            pltpu.SemaphoreType.DMA((2, seqs)),
+            pltpu.SemaphoreType.DMA((5,)),
         ],
         compiler_params=pltpu.CompilerParams(collective_id=1, has_side_effects=True),
         name="deliver",
@@ -452,8 +447,11 @@
 
     gain_full = spread(jnp.broadcast_to(gain, (slots, group)))
     lax.fori_loop(0, chunks, backward, 0)
+    lane = lax.broadcasted_iota(jnp.int32, head_ref.shape, 1)
+    total = jnp.zeros(head_ref.shape, F32)
     for i in range(3):
-        head_ref[i] = jnp.broadcast_to(jnp.sum(acc[i], axis=1, keepdims=True), head_ref.shape[1:])
+        total = jnp.where(lane == i, jnp.sum(acc[i], axis=1, keepdims=True), total)
+    head_ref[...] = total
 
 
 def mixer(pre, dy, par, hp):
@@ -465,7 +463,7 @@
             jax.ShapeDtypeStruct((pre.shape[0] - STATE, pre.shape[1]), BF16),
             jax.ShapeDtypeStruct((2, chunks // 2, pre.shape[0], group), BF16),
             jax.ShapeDtypeStruct((2, STATE, pre.shape[1]), F32),
-            jax.ShapeDtypeStruct((3, slots, 128), F32),
+            jax.ShapeDtypeStruct((slots, 128), F32),
         ),
         in_specs=[pl.BlockSpec(memory_space=pltpu.VMEM)] * 3,
         out_specs=(pl.BlockSpec(memory_space=pltpu.VMEM),) * 4,
@@ -548,8 +546,7 @@
         ],
         axis=1,
     )
-    sums_all = jnp.sum(sums_all.reshape(seqs, zeros, 3, slots, 128)[:, :, :, :hp, 0], axis=1)
-    head_grads = sums_all.transpose(1, 0, 2).reshape(3, seqs * hp)[:, :heads]
+    head_grads = sums_all[:, :hp, :3].transpose(2, 0, 1).reshape(3, seqs * hp)[:, :heads]
     return (token_grad[None], weight_grad, head_grads)
 
 

time: 133 us -> 124 us (0.932)
  Pallas kernels: 99.8 us -> 91 us
    pallas_call x1, Pallas kernels: 43.9 us -> 37.6 us  [deliver(): pl.pallas_call(functools.partial(deliver_kernel, seqs, zeros), out_shape=...]
    pallas_call x1, Pallas kernels: 5.65 us -> 3.22 us  [swap(): pl.pallas_call(swap_kernel, out_shape=(jax.ShapeDtypeStruct(split.shape[1...]
where the time goes in v4:
time: 124 us
  Pallas kernels  91 us (73%)
  matrix products  12.9 us (10%)
  local copies, waits for them, and re-layouts  12.4 us (10%)
  other arithmetic  6.71 us (5%)
    pallas_call x1, Pallas kernels, deliver(): pl.pallas_call(functools.partial(deliver_kernel, seqs, zeros), out_shape=...  37.6 us
    pallas_call x1, Pallas kernels, collect(): pl.pallas_call(functools.partial(collect_kernel, seqs, zeros), out_shape=...  31.2 us
    pallas_call x1, Pallas kernels, mixer(): pl.pallas_call(functools.partial(mixer_kernel, hp), out_shape=(jax.ShapeD...  19 us
    dot_general x1, matrix products, body(): lax.dot_general(columns, tokens, (((0,), (1,)), ((), ())), preferred_elem...  5.82 us
    dot_general x2, matrix products, back(): lax.dot_general(part, w, (((1,), (1,)), ((), ())), preferred_element_type...  4.41 us
    unnamed x46, local copies, waits for them, and re-layouts  4.31 us
    pallas_call x1, Pallas kernels, swap(): pl.pallas_call(swap_kernel, out_shape=(jax.ShapeDtypeStruct(split.shape[1...  3.22 us
    dot_general x1, matrix products, body(): lax.dot_general(tokens, grads, (((0,), (1,)), ((), ())), preferred_elemen...  2.65 us

profile of v4, /device:TPU:9, one launch (start us, length us, event | category | flops | bytes accessed | tf_op | source)
XLA Modules:
  0.0 124.0 jit_solution(9223203302645310440)
XLA Ops:
  0.6 0.0 copy-start
  0.6 0.0 slice-start
  0.7 1.0 slice.52
  1.7 0.9 slice.53
  2.6 0.1 constant_dynamic-slice_fusion
  2.7 0.0 copy-start.11
  2.8 0.1 constant_dynamic-slice_fusion.2
  2.9 0.1 pad.26.clone
  3.0 0.9 maximum_maximum_fusion.wgt
  3.9 1.1 copy.13
  5.0 31.2 %collect.1 = (bf16[8,128,1280]{2,1,0:T(8,128)(2,1)}, bf16[8,320,128]{2,1,0:T(8,128)(2,1)}, bf16[4,320,512]{2,1,0:T(8,128)(2,1)}, bf16[4,320,512]{2,1,0:T(8,128)(2,1)}) custom-call(bf16[128,1280]{1,0:T(8,128)(2,1)} %bitcast.47, bf16[8,320,128]{2,1,0:T(8,128)(2,1)} %bitcast.38, bf16[320,512]{1,0:T(8,128)(2,1)} %maximum_maximum_fusion.wgt), custom_call_target="tpu_custom_call" | custom-call | tf_op jit(solution)/shard_map/collect/pallas_call | solution.py:163
  36.2 1.4 %slice.68 = bf16[1280,320]{1,0:T(8,128)(2,1)S(1)} slice(bf16[1280,512]{1,0:T(8,128)(2,1)} %bitcast.42), slice={[0:1280], [0:320]} | slice | bytes 1638400 | tf_op jit(solution)/shard_map/slice | solution.py:518
  37.6 0.2 copy-done.7
  37.8 1.5 %broadcast_select_fusion.1 = (bf16[1280,128]{1,0:T(8,128)(2,1)S(1)}, bf16[1280,128]{1,0:T(8,128)(2,1)S(1)}) fusion(pred[]{:T(512)S(6)} %eq.4, bf16[1280,512]{1,0:T(8,128)(2,1)S(1)} %bitcast.39, bf16[1280,512]{1,0:T(8,128)(2,1)} %bitcast.43), kind=kLoop, calls=%fused_computation.26 | loop fusion | flops 327680 | bytes 1310721 | tf_op jit(solution)/shard_map/jit(_where)/select_n | solution.py:517
  39.3 0.0 copy-start.14
  39.4 0.0 copy-start.16
  39.4 1.4 %slice.71 = bf16[1280,64]{1,0:T(8,128)(2,1)S(1)} slice(bf16[1280,512]{1,0:T(8,128)(2,1)} %bitcast.44), slice={[0:1280], [448:512]} | slice | bytes 327680 | tf_op jit(solution)/shard_map/slice | solution.py:518
  40.7 0.0 copy-start.19
  40.8 5.8 %fusion.18.pre_ref = f32[640,1024]{1,0:T(8,128)} fusion(bf16[1024,1280]{1,0:T(8,128)(2,1)} %bitcast.49, bf16[1280,128]{1,0:T(8,128)(2,1)S(1)} %get-tuple-element.32, bf16[1280,128]{1,0:T(8,128)(2,1)S(1)} %get-tuple-element.31, bf16[1280,64]{1,0:T(8,128)(2,1)S(1)} %slice.71, bf16[1280,320]{1,0:T(8,128)(2,1)S(1)} %slice.68), kind=kOutput, calls=%fused_computation.28 | convolution fusion | flops 1684275200 | bytes 6881280 | tf_op jit(solution)/shard_map/dot_general | solution.py:520
  46.6 0.1 dynamic-slice_bitcast_fusion
  46.7 0.1 dynamic-slice_bitcast_fusion.2
  46.8 0.1 broadcast_in_dim.13.par_ref
  46.9 19.0 %mixer.1 = (bf16[512,1024]{1,0:T(8,128)(2,1)S(1)}, bf16[2,4,640,128]{3,2,1,0:T(8,128)(2,1)S(1)}, f32[2,128,1024]{2,1,0:T(8,128)S(1)}, f32[8,128]{1,0:T(8,128)S(1)}) custom-call(f32[640,1024]{1,0:T(8,128)} %fusion.18.pre_ref, bf16[8,320,128]{2,1,0:T(8,128)(2,1)S(1)} %copy-done.5, f32[3,8,128]{2,1,0:T(8,128)S(1)} %broadcast_in_dim.13.par_ref), custom_call_target="tpu_custom_call" | custom-call | tf_op jit(solution)/shard_map/mixer/pallas_call | solution.py:460
  65.9 1.0 copy-done.1
  66.9 1.1 copy-done.3
  68.0 0.6 copy-done.6
  68.6 3.2 %swap.1 = (bf16[4,640,128]{2,1,0:T(8,128)(2,1)}, f32[128,1024]{1,0:T(8,128)}) custom-call(bf16[2,4,640,128]{3,2,1,0:T(8,128)(2,1)} %copy-done.3, f32[2,128,1024]{2,1,0:T(8,128)} %copy-done.1), custom_call_target="tpu_custom_call" | custom-call | tf_op jit(solution)/shard_map/swap/pallas_call | solution.py:203
  71.8 1.3 %fusion.16 = bf16[128,1024]{1,0:T(8,128)(2,1)S(1)} fusion(f32[128,1024]{1,0:T(8,128)} %get-tuple-element.24, f32[2,128,1024]{2,1,0:T(8,128)S(1)} %copy-done.2, s32[]{:T(128)S(6)} %select_n.34), kind=kLoop, calls=%fused_computation.22 | loop fusion | flops 262144 | bytes 1310724 | tf_op jit(solution)/shard_map/convert_element_type | solution.py:524
  73.2 0.5 copy-done.21
  73.7 0.0 copy-start.17
  73.8 2.7 %convolution_convert_fusion = bf16[1280,512]{1,0:T(8,128)(2,1)} fusion(bf16[1024,1280]{1,0:T(8,128)(2,1)S(1)} %bitcast.50, bf16[64,1024]{1,0:T(8,128)(2,1)S(1)} %slice.62, bf16[128,1024]{1,0:T(8,128)(2,1)S(1)} %fusion.16, bf16[320,1024]{1,0:T(8,128)(2,1)S(1)} %slice.61), kind=kOutput, calls=%fused_computation.2 | convolution fusion | flops 1345978368 | bytes 4980736 | tf_op jit(solution)/shard_map/dot_general | solution.py:530
  76.4 1.7 %fusion.7 = f32[4,128,1280]{2,1,0:T(8,128)S(1)} fusion(bf16[2,4,640,128]{3,2,1,0:T(8,128)(2,1)S(1)} %copy-done.4, bf16[1280,128]{1,0:T(8,128)(2,1)S(1)} %copy-done.17, bf16[1280,128]{1,0:T(8,128)(2,1)S(1)} %copy-done.15, bf16[1280,64]{1,0:T(8,128)(2,1)S(1)} %copy-done.13, bf16[1280,320]{1,0:T(8,128)(2,1)S(1)} %copy-done.10), kind=kOutput, calls=%fused_computation.12 | convolution fusion | flops 845414400 | bytes 5242880 | tf_op jit(solution)/shard_map/dot_general | solution.py:527
  78.1 0.1 slice.72
  78.2 0.2 slice.73
  78.4 0.8 copy-done.22
  79.2 2.8 %fusion.tok = bf16[4,128,1280]{2,1,0:T(8,128)(2,1)} fusion(f32[4,128,1280]{2,1,0:T(8,128)S(1)} %fusion.7, bf16[4,640,128]{2,1,0:T(8,128)(2,1)S(1)} %copy-done.22, bf16[1280,128]{1,0:T(8,128)(2,1)S(1)} %copy-done.17, bf16[1280,128]{1,0:T(8,128)(2,1)S(1)} %copy-done.15, bf16[1280,64]{1,0:T(8,128)(2,1)S(1)} %slice.73, bf16[1280,320]{1,0:T(8,128)(2,1)S(1)} %slice.72), kind=kOutput, calls=%fused_computation.1 | convolution fusion | flops 846725120 | bytes 6225920 | tf_op jit(solution)/shard_map/dot_general | solution.py:527
  81.9 37.6 %deliver.1 = (bf16[4,128,1280]{2,1,0:T(8,128)(2,1)}, bf16[8,40,512]{2,1,0:T(8,128)(2,1)}, f32[8,8,128]{2,1,0:T(8,128)}) custom-call(bf16[4,128,1280]{2,1,0:T(8,128)(2,1)} %fusion.tok, bf16[8,4,40,512]{3,2,1,0:T(8,128)(2,1)} %bitcast.45, f32[8,128]{1,0:T(8,128)} %copy-done.6), custom_call_target="tpu_custom_call" | custom-call | tf_op jit(solution)/shard_map/deliver/pallas_call | solution.py:292
  119.5 1.1 fusion.24
  120.7 0.1 copy.16
  120.8 0.1 reshape.36
  120.9 0.1 slice.75
  121.0 0.1 copy.17
  121.2 0.1 copy.18
  121.2 0.1 slice_reduce_fusion.1
  121.4 0.8 pad_maximum_fusion.4
  122.2 1.0 reduce_sum.30
  123.2 0.1 copy.19
  123.3 0.7 reshape.38
  (43 shorter events, 0.2 us)
Async XLA Ops:
  0.6 46.1 %copy-start = (f32[40]{0:T(128)S(1)}, f32[40]{0:T(128)}, u32[]{:S(2)}) copy-start(f32[40]{0:T(128)} %param.9) | copy-start | bytes 484
  0.6 2.1 %slice-start = ((bf16[320,2856]{1,0:T(8,128)(2,1)}), bf16[320,2560]{1,0:T(8,128)(2,1)S(1)}, s32[]{:S(2)}) async-start(bf16[320,2856]{1,0:T(8,128)(2,1)} %param.8), calls=%async_computation | async-start | bytes 3276800 | tf_op jit(solution)/shard_map/slice | solution.py:501
  2.7 1.1 copy-start.11
  36.2 1.6 %copy-start.7 = (bf16[4,320,512]{2,1,0:T(8,128)(2,1)S(1)}, bf16[4,320,512]{2,1,0:T(8,128)(2,1)}, u32[]{:S(2)}) copy-start(bf16[4,320,512]{2,1,0:T(8,128)(2,1)} %get-tuple-element.17) | copy-start | bytes 3932164
  37.6 9.0 %copy-start.9 = (bf16[1280,320]{1,0:T(8,128)(2,1)}, bf16[1280,320]{1,0:T(8,128)(2,1)S(1)}, u32[]{:S(2)}) copy-start(bf16[1280,320]{1,0:T(8,128)(2,1)S(1)} %slice.68) | copy-start | bytes 2457604
  39.3 7.3 %copy-start.14 = (bf16[1280,128]{1,0:T(8,128)(2,1)}, bf16[1280,128]{1,0:T(8,128)(2,1)S(1)}, u32[]{:S(2)}) copy-start(bf16[1280,128]{1,0:T(8,128)(2,1)S(1)} %get-tuple-element.31) | copy-start | bytes 983044
  39.4 7.2 %copy-start.16 = (bf16[1280,128]{1,0:T(8,128)(2,1)}, bf16[1280,128]{1,0:T(8,128)(2,1)S(1)}, u32[]{:S(2)}) copy-start(bf16[1280,128]{1,0:T(8,128)(2,1)S(1)} %get-tuple-element.32) | copy-start | bytes 983044
  40.7 5.9 %copy-start.12 = (bf16[1280,64]{1,0:T(8,128)(2,1)}, bf16[1280,64]{1,0:T(8,128)(2,1)S(1)}, u32[]{:S(2)}) copy-start(bf16[1280,64]{1,0:T(8,128)(2,1)S(1)} %slice.71) | copy-start | bytes 491524
  40.7 5.9 %copy-start.19 = (f32[40]{0:T(128)S(1)}, f32[40]{0:T(128)}, u32[]{:S(2)}) copy-start(f32[40]{0:T(128)} %param.11) | copy-start | bytes 484
  40.8 5.9 %copy-start.20 = (f32[40]{0:T(128)S(1)}, f32[40]{0:T(128)}, u32[]{:S(2)}) copy-start(f32[40]{0:T(128)} %param.10) | copy-start | bytes 484
  40.8 6.1 %copy-start.5 = (bf16[8,320,128]{2,1,0:T(8,128)(2,1)S(1)}, bf16[8,320,128]{2,1,0:T(8,128)(2,1)}, u32[]{:S(2)}) copy-start(bf16[8,320,128]{2,1,0:T(8,128)(2,1)} %get-tuple-element.19.dy_ref) | copy-start | bytes 1966084
  65.9 1.0 copy-start.1
  66.9 1.1 copy-start.3
  68.0 0.6 copy-start.6
  68.6 3.2 %copy-start.2 = (f32[2,128,1024]{2,1,0:T(8,128)S(1)}, f32[2,128,1024]{2,1,0:T(8,128)}, u32[]{:S(2)}) copy-start(f32[2,128,1024]{2,1,0:T(8,128)} %copy-done.1) | copy-start | bytes 3145732
  71.8 1.9 %copy-start.21 = (bf16[8,128,1280]{2,1,0:T(8,128)(2,1)S(1)}, bf16[8,128,1280]{2,1,0:T(8,128)(2,1)}, u32[]{:S(2)}) copy-start(bf16[8,128,1280]{2,1,0:T(8,128)(2,1)} %get-tuple-element.18) | copy-start | bytes 7864324
  73.7 2.7 %copy-start.4 = (bf16[2,4,640,128]{3,2,1,0:T(8,128)(2,1)S(1)}, bf16[2,4,640,128]{3,2,1,0:T(8,128)(2,1)}, u32[]{:S(2)}) copy-start(bf16[2,4,640,128]{3,2,1,0:T(8,128)(2,1)} %copy-done.3) | copy-start | bytes 3932164
  73.7 2.7 %copy-start.10 = (bf16[1280,320]{1,0:T(8,128)(2,1)S(1)}, bf16[1280,320]{1,0:T(8,128)(2,1)}, u32[]{:S(2)}) copy-start(bf16[1280,320]{1,0:T(8,128)(2,1)} %copy-done.9) | copy-start | bytes 2457604
  73.7 2.7 %copy-start.13 = (bf16[1280,64]{1,0:T(8,128)(2,1)S(1)}, bf16[1280,64]{1,0:T(8,128)(2,1)}, u32[]{:S(2)}) copy-start(bf16[1280,64]{1,0:T(8,128)(2,1)} %copy-done.12) | copy-start | bytes 491524
  73.7 2.7 %copy-start.15 = (bf16[1280,128]{1,0:T(8,128)(2,1)S(1)}, bf16[1280,128]{1,0:T(8,128)(2,1)}, u32[]{:S(2)}) copy-start(bf16[1280,128]{1,0:T(8,128)(2,1)} %copy-done.14) | copy-start | bytes 983044
  73.7 2.7 %copy-start.17 = (bf16[1280,128]{1,0:T(8,128)(2,1)S(1)}, bf16[1280,128]{1,0:T(8,128)(2,1)}, u32[]{:S(2)}) copy-start(bf16[1280,128]{1,0:T(8,128)(2,1)} %copy-done.16) | copy-start | bytes 983044
  78.1 1.1 copy-start.22
  120.6 1.6 %copy-start.8 = (bf16[4,128,1280]{2,1,0:T(8,128)(2,1)S(1)}, bf16[4,128,1280]{2,1,0:T(8,128)(2,1)}, u32[]{:S(2)}) copy-start(bf16[4,128,1280]{2,1,0:T(8,128)(2,1)} %get-tuple-element.26) | copy-start | bytes 3932164
  120.9 2.3 %copy-start.18 = (f32[8,8,128]{2,1,0:T(8,128)S(1)}, f32[8,8,128]{2,1,0:T(8,128)}, u32[]{:S(2)}) copy-start(f32[8,8,128]{2,1,0:T(8,128)} %get-tuple-element.28) | copy-start | bytes 98308

commit v5 on v4

--- a/solution.py
+++ b/solution.py
@@ -315,9 +315,9 @@
     )(tok, wgt, head)
 
 
-def mixer_kernel(hp, pre_ref, dy_ref, par_ref, g_ref, split_ref, maps_ref, head_ref, states, grad, acc):
+def mixer_kernel(hp, pre_ref, other_ref, dy_ref, par_ref, g_ref, split_ref, maps_ref, head_ref, states, grad, acc):
     chunks, inner, group = dy_ref.shape
-    top = inner + 2 * STATE
+    top = inner + STATE
     slots = acc.shape[1]
     core = lax.rem(lax.axis_index("seq"), 2)
     bias = par_ref[0][:, :1]
@@ -346,7 +346,10 @@
         at = pl.ds(pl.multiple_of(k * group, group), group)
         pre = pre_ref[:inner, at]
         sig = jax.nn.sigmoid(pre)
-        maps = pre_ref[inner:top, at]
+        here, there = pre_ref[inner:top, at], other_ref[:, at]
+        maps = jnp.concatenate(
+            [jnp.where(core == 0, here, there), jnp.where(core == 0, there, here)], axis=0
+        )
         map_sig = jax.nn.sigmoid(maps)
         raw = pre_ref[top : top + slots, at] + bias
         step = jax.nn.softplus(raw)
@@ -424,22 +427,22 @@
 
         slope = sig * (1.0 + pre * (1.0 - sig))
         map_slope = map_sig * (1.0 + maps * (1.0 - map_sig))
-        rest = g_ref.shape[0] - inner - STATE - slots
+        rest = g_ref.shape[0] - top - slots
+        d_in = d_in * map_slope[:STATE]
+        d_out = d_out * map_slope[STATE:]
         rounded = jnp.concatenate(
             [
                 (du * spread(step) + dy * gain_full) * slope,
-                jnp.concatenate([d_in, d_out], axis=0) * map_slope,
+                jnp.where(core == 0, d_in, d_out),
                 d_raw,
                 jnp.zeros((rest, group), F32),
             ],
             axis=0,
         ).astype(BF16)
-        maps_ref[0, :, at] = d_in * map_slope[:STATE]
-        maps_ref[1, :, at] = d_out * map_slope[STATE:]
-        g_ref[:inner, at] = rounded[:inner]
-        g_ref[inner : inner + STATE, at] = jnp.zeros((STATE, group), BF16)
-        g_ref[inner + STATE :, at] = rounded[top:]
+        g_ref[:, at] = rounded
         split_ref[lax.rem(k + core, 2), k // 2] = rounded
+        maps_ref[0, :, at] = d_in
+        maps_ref[1, :, at] = d_out
         acc[0] += d_raw
         acc[1] += d_log * (rate * step)
         acc[2] += gather_rows(dy * x)
@@ -454,18 +457,18 @@
     head_ref[...] = total
 
 
-def mixer(pre, dy, par, hp):
+def mixer(pre, other, dy, par, hp):
     chunks, inner, group = dy.shape
     slots = par.shape[1]
     return pl.pallas_call(
         functools.partial(mixer_kernel, hp),
         out_shape=(
-            jax.ShapeDtypeStruct((pre.shape[0] - STATE, pre.shape[1]), BF16),
+            jax.ShapeDtypeStruct(pre.shape, BF16),
             jax.ShapeDtypeStruct((2, chunks // 2, pre.shape[0], group), BF16),
             jax.ShapeDtypeStruct((2, STATE, pre.shape[1]), F32),
             jax.ShapeDtypeStruct((slots, 128), F32),
         ),
-        in_specs=[pl.BlockSpec(memory_space=pltpu.VMEM)] * 3,
+        in_specs=[pl.BlockSpec(memory_space=pltpu.VMEM)] * 4,
         out_specs=(pl.BlockSpec(memory_space=pltpu.VMEM),) * 4,
         scratch_shapes=[
             pltpu.VMEM((chunks, inner, STATE), F32),
@@ -474,7 +477,7 @@
         ],
         compiler_params=pltpu.CompilerParams(vmem_limit_bytes=48 * 1024 * 1024),
         name="mixer",
-    )(pre, dy, par)
+    )(pre, other, dy, par)
 
 
 def body(seqs, zeros, hidden, output_grad, input_weight, step_bias, decay_log, skip_gain):
@@ -513,12 +516,11 @@
     tokens = tokens.reshape(seqs * length, model)
     columns = columns.reshape(model, width)
     beside = beside.reshape(model, width)
-    here, there = columns[:, inner:mine], beside[:, inner:mine]
-    both = [jnp.where(core == 0, here, there), jnp.where(core == 0, there, here)]
-    columns = jnp.concatenate([columns[:, :inner]] + both + [columns[:, mine:]], axis=1)
-    beside = jnp.concatenate([beside[:, :inner]] + both + [beside[:, mine:]], axis=1)
     pre = lax.dot_general(columns, tokens, (((0,), (1,)), ((), ())), preferred_element_type=F32)
-    grads, split, maps, sums = mixer(pre, dy, par, hp)
+    other_pre = lax.dot_general(
+        beside[:, inner:mine], tokens, (((0,), (1,)), ((), ())), preferred_element_type=F32
+    )
+    grads, split, maps, sums = mixer(pre, other_pre, dy, par, hp)
     other, other_map = swap(split, maps)
     pair_map = lax.dynamic_index_in_dim(maps, core, 0, False) + other_map
     grads = jnp.concatenate([grads[:inner], pair_map.astype(BF16), grads[mine:]], axis=0)
@@ -526,7 +528,17 @@
     def back(part, w):
         return lax.dot_general(part, w, (((1,), (1,)), ((), ())), preferred_element_type=F32)
 
-    token_part = (back(split[0], columns) + back(other, beside)).astype(BF16)
+    def parity(m):
+        m = m.reshape(STATE, seqs // 2, 2, length)
+        return lax.dynamic_index_in_dim(m, core, 2, False).transpose(1, 0, 2)
+
+    def filled(part, middle):
+        return jnp.concatenate([part[:, :inner], middle.astype(BF16), part[:, mine:]], axis=1)
+
+    first = filled(split[0], parity(pair_map))
+    rest_map = lax.dynamic_index_in_dim(maps, 1 - core, 0, False)
+    second = filled(other, other[:, inner:mine].astype(F32) + parity(rest_map))
+    token_part = (back(first, columns) + back(second, beside)).astype(BF16)
     weight_part = lax.dot_general(
         tokens, grads, (((0,), (1,)), ((), ())), preferred_element_type=F32
     ).astype(BF16)

time: 124 us -> 121 us (0.976)
  local copies, waits for them, and re-layouts: 12.4 us -> 9.65 us
    dot_general x0 -> x1, matrix products: none -> 3.3 us  [body(): lax.dot_general(beside[:, inner:mine], tokens, (((0,), (1,)), ((), ())),...]
    slice x4, local copies, waits for them, and re-layouts: 3.02 us -> 0.06 us  [the longest x2 0.05 us: filled(): part[:, :inner]]
    dot_general x2, matrix products: 4.41 us -> 2.88 us  [back(): lax.dot_general(part, w, (((1,), (1,)), ((), ())), preferred_element_type...]
    select_n x1 -> x0, other arithmetic: 1.53 us -> none  [body(): jnp.where(core == 0, here, there)]
    dot_general x1, matrix products: 5.82 us -> 4.29 us  [body(): lax.dot_general(columns, tokens, (((0,), (1,)), ((), ())), preferred_elem...]
    add x0 -> x1, other arithmetic: none -> 1.27 us  [body(): pair_map = lax.dynamic_index_in_dim(maps, core, 0, False) + other_map]
    unnamed x46 -> x35, local copies, waits for them, and re-layouts: 4.31 us -> 3.7 us
where the time goes in v5:
time: 121 us
  Pallas kernels  90.5 us (75%)
  matrix products  13.1 us (11%)
  local copies, waits for them, and re-layouts  9.65 us (8%)
  other arithmetic  6.28 us (5%)
    pallas_call x1, Pallas kernels, deliver(): pl.pallas_call(functools.partial(deliver_kernel, seqs, zeros), out_shape=...  37.6 us
    pallas_call x1, Pallas kernels, collect(): pl.pallas_call(functools.partial(collect_kernel, seqs, zeros), out_shape=...  31.2 us
    pallas_call x1, Pallas kernels, mixer(): pl.pallas_call(functools.partial(mixer_kernel, hp), out_shape=(jax.ShapeD...  18.7 us
    dot_general x1, matrix products, body(): lax.dot_general(columns, tokens, (((0,), (1,)), ((), ())), preferred_elem...  4.29 us
    unnamed x35, local copies, waits for them, and re-layouts  3.7 us
    dot_general x1, matrix products, body(): lax.dot_general(beside[:, inner:mine], tokens, (((0,), (1,)), ((), ())),...  3.3 us
    pallas_call x1, Pallas kernels, swap(): pl.pallas_call(swap_kernel, out_shape=(jax.ShapeDtypeStruct(split.shape[1...  3.04 us
    dot_general x2, matrix products, back(): lax.dot_general(part, w, (((1,), (1,)), ((), ())), preferred_element_type...  2.88 us

profile of v5, /device:TPU:9, one launch (start us, length us, event | category | flops | bytes accessed | tf_op | source)
XLA Modules:
  0.0 120.6 jit_solution(6540767198719107355)
XLA Ops:
  0.6 0.0 copy-start
  0.6 0.0 slice-start
  0.7 1.0 slice.52
  1.7 0.9 slice.53
  2.6 0.1 constant_dynamic-slice_fusion.3
  2.7 0.0 copy-start.12
  2.8 0.1 constant_dynamic-slice_fusion.5
  2.9 0.1 pad.24.clone
  3.0 0.9 maximum_maximum_fusion.wgt
  3.9 1.1 copy.14
  5.0 31.2 %collect.1 = (bf16[8,128,1280]{2,1,0:T(8,128)(2,1)}, bf16[8,320,128]{2,1,0:T(8,128)(2,1)}, bf16[4,320,512]{2,1,0:T(8,128)(2,1)}, bf16[4,320,512]{2,1,0:T(8,128)(2,1)}) custom-call(bf16[128,1280]{1,0:T(8,128)(2,1)} %bitcast.60, bf16[8,320,128]{2,1,0:T(8,128)(2,1)} %bitcast.51, bf16[320,512]{1,0:T(8,128)(2,1)} %maximum_maximum_fusion.wgt), custom_call_target="tpu_custom_call" | custom-call | tf_op jit(solution)/shard_map/collect/pallas_call | solution.py:163
  36.2 3.3 %fusion.17.other_ref = f32[128,1024]{1,0:T(8,128)S(1)} fusion(bf16[1024,1280]{1,0:T(8,128)(2,1)} %bitcast.48, bf16[1280,512]{1,0:T(8,128)(2,1)} %bitcast.52), kind=kOutput, calls=%fused_computation.22 | convolution fusion | flops 335544320 | bytes 3473408 | tf_op jit(solution)/shard_map/dot_general | solution.py:520
  39.5 0.0 copy-start.15
  39.5 0.0 copy-start.16
  39.5 0.0 copy-start.5
  39.5 4.3 %fusion.25.pre_ref = f32[512,1024]{1,0:T(8,128)} fusion(bf16[1280,512]{1,0:T(8,128)(2,1)} %bitcast.55, bf16[1024,1280]{1,0:T(8,128)(2,1)S(1)} %bitcast.49), kind=kOutput, calls=%fused_computation.49 | convolution fusion | flops 1342177280 | bytes 6029312 | tf_op jit(solution)/shard_map/dot_general | solution.py:519
  43.8 0.1 dynamic-slice_bitcast_fusion
  43.9 0.1 dynamic-slice_bitcast_fusion.2
  44.0 0.1 broadcast_in_dim.13.par_ref
  44.1 18.7 %mixer.1 = (bf16[512,1024]{1,0:T(8,128)(2,1)S(1)}, bf16[2,4,512,128]{3,2,1,0:T(8,128)(2,1)S(1)}, f32[2,128,1024]{2,1,0:T(8,128)S(1)}, f32[8,128]{1,0:T(8,128)S(1)}) custom-call(f32[512,1024]{1,0:T(8,128)} %fusion.25.pre_ref, f32[128,1024]{1,0:T(8,128)S(1)} %fusion.17.other_ref, bf16[8,320,128]{2,1,0:T(8,128)(2,1)S(1)} %copy-done.5, ...), custom_call_target="tpu_custom_call" | custom-call | tf_op jit(solution)/shard_map/mixer/pallas_call | solution.py:463
  62.8 1.0 copy-done.1
  63.8 1.0 copy-done.3
  64.7 0.6 copy-done.6
  65.3 3.0 %swap.1 = (bf16[4,512,128]{2,1,0:T(8,128)(2,1)}, f32[128,1024]{1,0:T(8,128)}) custom-call(bf16[2,4,512,128]{3,2,1,0:T(8,128)(2,1)} %copy-done.3, f32[2,128,1024]{2,1,0:T(8,128)} %copy-done.1), custom_call_target="tpu_custom_call" | custom-call | tf_op jit(solution)/shard_map/swap/pallas_call | solution.py:203
  68.4 1.3 %bitcast_add_fusion = bf16[128,1024]{1,0:T(8,128)(2,1)S(1)} fusion(f32[128,1024]{1,0:T(8,128)} %get-tuple-element.22, f32[2,128,1024]{2,1,0:T(8,128)S(1)} %copy-done.2, s32[]{:T(128)S(6)} %select_n.25), kind=kLoop, calls=%fused_computation.19 | loop fusion | flops 262144 | bytes 1310724 | tf_op jit(solution)/shard_map/add | solution.py:525
  69.7 0.5 copy-done.8
  70.3 2.7 %convolution_convert_fusion = bf16[1280,512]{1,0:T(8,128)(2,1)} fusion(bf16[1024,1280]{1,0:T(8,128)(2,1)S(1)} %bitcast.50, bf16[64,1024]{1,0:T(8,128)(2,1)S(1)} %slice.62, bf16[128,1024]{1,0:T(8,128)(2,1)S(1)} %bitcast_add_fusion, bf16[320,1024]{1,0:T(8,128)(2,1)S(1)} %slice.61), kind=kOutput, calls=%fused_computation.1 | convolution fusion | flops 1345978368 | bytes 4980736 | tf_op jit(solution)/shard_map/dot_general | solution.py:542
  73.0 0.2 copy.17
  73.3 0.1 copy.18
  73.4 1.1 fusion.19
  74.5 0.2 reshape.43
  74.7 0.3 constant_dynamic-slice_fusion.2
  75.1 0.9 fusion.6
  76.0 0.1 copy-done.13
  76.2 0.4 copy-done.9
  76.6 2.0 %fusion.tok = bf16[4,128,1280]{2,1,0:T(8,128)(2,1)} fusion(f32[4,128,1280]{2,1,0:T(8,128)S(1)} %fusion.6, bf16[1280,512,1]{1,0,2:T(8,128)(2,1)S(1)} %bitcast.53, bf16[4,64,128]{2,1,0:T(8,128)(2,1)S(1)} %slice.60, bf16[4,128,128]{2,1,0:T(8,128)(2,1)S(1)} %fusion.19, bf16[4,320,128]{2,1,0:T(8,128)(2,1)S(1)} %slice.58), kind=kOutput, calls=%fused_computation.2 | convolution fusion | flops 673972224 | bytes 5767168 | tf_op jit(solution)/shard_map/dot_general | solution.py:529
  78.6 37.6 %deliver.1 = (bf16[4,128,1280]{2,1,0:T(8,128)(2,1)}, bf16[8,40,512]{2,1,0:T(8,128)(2,1)}, f32[8,8,128]{2,1,0:T(8,128)}) custom-call(bf16[4,128,1280]{2,1,0:T(8,128)(2,1)} %fusion.tok, bf16[8,4,40,512]{3,2,1,0:T(8,128)(2,1)} %bitcast.54, f32[8,128]{1,0:T(8,128)} %copy-done.6), custom_call_target="tpu_custom_call" | custom-call | tf_op jit(solution)/shard_map/deliver/pallas_call | solution.py:292
  116.2 1.1 fusion.24
  117.3 0.1 copy.20
  117.4 0.1 reshape.46
  117.6 0.1 slice.72
  117.7 0.1 copy.21
  117.8 0.1 copy.22
  117.9 0.1 slice_reduce_fusion.1
  118.0 0.8 pad_maximum_fusion
  118.8 1.0 reduce_sum.30
  119.8 0.1 copy.23
  120.0 0.7 reshape.48
  (40 shorter events, 0.4 us)
Async XLA Ops:
  0.6 43.3 %copy-start = (f32[40]{0:T(128)S(1)}, f32[40]{0:T(128)}, u32[]{:S(2)}) copy-start(f32[40]{0:T(128)} %param.9) | copy-start | bytes 484
  0.6 2.1 %slice-start = ((bf16[320,2856]{1,0:T(8,128)(2,1)}), bf16[320,2560]{1,0:T(8,128)(2,1)S(1)}, s32[]{:S(2)}) async-start(bf16[320,2856]{1,0:T(8,128)(2,1)} %param.8), calls=%async_computation | async-start | bytes 3276800 | tf_op jit(solution)/shard_map/slice | solution.py:504
  2.7 1.1 copy-start.12
  36.2 3.3 %copy-start.7 = (bf16[8,128,1280]{2,1,0:T(8,128)(2,1)S(1)}, bf16[8,128,1280]{2,1,0:T(8,128)(2,1)}, u32[]{:S(2)}) copy-start(bf16[8,128,1280]{2,1,0:T(8,128)(2,1)} %get-tuple-element.17) | copy-start | bytes 7864324
  39.5 4.3 %copy-start.15 = (f32[40]{0:T(128)S(1)}, f32[40]{0:T(128)}, u32[]{:S(2)}) copy-start(f32[40]{0:T(128)} %param.11) | copy-start | bytes 484
  39.5 4.3 %copy-start.16 = (f32[40]{0:T(128)S(1)}, f32[40]{0:T(128)}, u32[]{:S(2)}) copy-start(f32[40]{0:T(128)} %param.10) | copy-start | bytes 484
  39.5 4.5 %copy-start.5 = (bf16[8,320,128]{2,1,0:T(8,128)(2,1)S(1)}, bf16[8,320,128]{2,1,0:T(8,128)(2,1)}, u32[]{:S(2)}) copy-start(bf16[8,320,128]{2,1,0:T(8,128)(2,1)} %get-tuple-element.19.dy_ref) | copy-start | bytes 1966084
  62.8 1.0 copy-start.1
  63.8 1.0 copy-start.3
  64.7 0.6 copy-start.6
  65.3 3.1 %copy-start.2 = (f32[2,128,1024]{2,1,0:T(8,128)S(1)}, f32[2,128,1024]{2,1,0:T(8,128)}, u32[]{:S(2)}) copy-start(f32[2,128,1024]{2,1,0:T(8,128)} %copy-done.1) | copy-start | bytes 3145732
  68.4 1.9 %copy-start.8 = (bf16[8,128,1280]{2,1,0:T(8,128)(2,1)S(1)}, bf16[8,128,1280]{2,1,0:T(8,128)(2,1)}, u32[]{:S(2)}) copy-start(bf16[8,128,1280]{2,1,0:T(8,128)(2,1)} %get-tuple-element.17) | copy-start | bytes 7864324
  73.0 2.0 %copy-start.4 = (bf16[2,4,512,128]{3,2,1,0:T(8,128)(2,1)S(1)}, bf16[2,4,512,128]{3,2,1,0:T(8,128)(2,1)}, u32[]{:S(2)}) copy-start(bf16[2,4,512,128]{3,2,1,0:T(8,128)(2,1)} %copy-done.3) | copy-start | bytes 3145732
  73.3 1.8 %copy-start.11 = (bf16[4,320,512]{2,1,0:T(8,128)(2,1)S(1)}, bf16[4,320,512]{2,1,0:T(8,128)(2,1)}, u32[]{:S(2)}) copy-start(bf16[4,320,512]{2,1,0:T(8,128)(2,1)} %get-tuple-element.16) | copy-start | bytes 3932164
  75.1 1.0 copy-start.13
  75.1 1.5 %copy-start.9 = (bf16[4,320,512]{2,1,0:T(8,128)(2,1)S(1)}, bf16[4,320,512]{2,1,0:T(8,128)(2,1)}, u32[]{:S(2)}) copy-start(bf16[4,320,512]{2,1,0:T(8,128)(2,1)} %get-tuple-element.18) | copy-start | bytes 3932164
  117.3 1.6 %copy-start.10 = (bf16[4,128,1280]{2,1,0:T(8,128)(2,1)S(1)}, bf16[4,128,1280]{2,1,0:T(8,128)(2,1)}, u32[]{:S(2)}) copy-start(bf16[4,128,1280]{2,1,0:T(8,128)(2,1)} %get-tuple-element.26) | copy-start | bytes 3932164
  117.6 2.3 %copy-start.14 = (f32[8,8,128]{2,1,0:T(8,128)S(1)}, f32[8,8,128]{2,1,0:T(8,128)}, u32[]{:S(2)}) copy-start(f32[8,8,128]{2,1,0:T(8,128)} %get-tuple-element.28) | copy-start | bytes 98308
